TPU v7x, 32 devices: a whole 2x2x4 slice. The times are simulated.
32 devices in a mesh: ctx: 8 (over z, x), head: 4 (over y, core).
Axes of the slice: x: 2, y: 2, z: 4, core: 2. Of those that a mesh axis runs over, the one named last changes fastest.
Arguments:
- queries: bfloat16 [2048, 8192], P('ctx', 'head'), may hold values from -20 to 20
- keys: bfloat16 [2048, 1024], P('ctx', 'head'), may hold values from -4 to 4
- values: bfloat16 [2048, 1024], P('ctx', 'head'), may hold values from -6 to 6
- grad_out: bfloat16 [2048, 8192], P('ctx', 'head'), may hold values from -6 to 6
- key_blocks: int32 [16, 6], replicated, may hold values from 0 to 15, as said below
- key_count: int32 [16], replicated, may hold values from 2 to 6
Outputs:
- attended: bfloat16 [2048, 8192], P('ctx', 'head')
- grad_q: bfloat16 [2048, 8192], P('ctx', 'head')
- grad_k: bfloat16 [2048, 1024], P('ctx', 'head')
- grad_v: bfloat16 [2048, 1024], P('ctx', 'head')
Inputs may be any that keep to these rules, and one draw needn't show every extreme that they name: `key_blocks`: the listed key blocks of block b lie outside the range of 2 blocks that holds b (ranges begin at multiples of 2), each in a different range. Over the used slots of all query blocks of one range, at most 2 name blocks of any one other range; in every draw the query blocks of one range use all their 6 slots, so that this most and 12 used slots of one range are reached.
All inputs are finite; a program needn't handle non-finite values.
Results may differ from a plain program's by a relative error of at most 0.034.
Values may be sent and summed in bfloat16 or wider, within the bound.
No kernel may reach another device: no remote copies, remote signals or barrier semaphores. Data moves between devices by JAX's collectives and lax.ppermute only.
A program may use at most 64 MiB of HBM per device.

v0:
```python
import math

import jax
import jax.numpy as jnp
from jax import lax
from jax.sharding import PartitionSpec as P

QH = 64
KVH = 8
DH = 128
BLOCK = 128
KSLOTS = 6


def attend(q_blk, o_blk, near_k, near_v, column, scaling):
    scores = (
        jnp.einsum("qhgd,khd->hgqk", q_blk, near_k, preferred_element_type=jnp.float32) * scaling
    )
    scores = jnp.where(column, scores, -1e30)
    row_max = jnp.max(scores, axis=-1, keepdims=True)
    expo_terms = jnp.where(column, jnp.exp(scores - row_max), 0.0)
    prob_rows = expo_terms / jnp.sum(expo_terms, axis=-1, keepdims=True)
    weights = prob_rows.astype(jnp.bfloat16)
    attended = jnp.einsum(
        "hgqk,khd->qhgd", weights, near_v, preferred_element_type=jnp.float32
    ).astype(jnp.bfloat16)
    delta_rows = jnp.sum(o_blk.astype(jnp.float32) * attended.astype(jnp.float32), axis=-1)
    grad_p = jnp.einsum("qhgd,khd->hgqk", o_blk, near_v, preferred_element_type=jnp.float32)
    grad_s = (
        prob_rows * (grad_p - jnp.transpose(delta_rows, (1, 2, 0))[..., None]) * scaling
    ).astype(jnp.bfloat16)
    grad_q = jnp.einsum(
        "hgqk,khd->qhgd", grad_s, near_k, preferred_element_type=jnp.float32
    ).astype(jnp.bfloat16)
    part_k = jnp.einsum("hgqk,qhgd->khd", grad_s, q_blk, preferred_element_type=jnp.float32)
    part_v = jnp.einsum("hgqk,qhgd->khd", weights, o_blk, preferred_element_type=jnp.float32)
    return (attended, grad_q, part_k, part_v)


def local(queries, keys, values, grad_out, key_blocks, key_count):
    q_loc, o_loc, k_loc, v_loc = (queries, grad_out, keys, values)
    contexts = lax.axis_size("ctx")
    position = lax.axis_index("ctx")
    row_count = q_loc.shape[0]
    blk_dev = row_count // BLOCK
    heads_loc = k_loc.shape[1] // DH
    group_size = QH // KVH
    tile_size = BLOCK * heads_loc * DH
    entries = blk_dev * KSLOTS
    slots_peer = (entries + contexts - 2) // (contexts - 1)
    key_width = (KSLOTS + 1) * BLOCK
    scaling = 1.0 / math.sqrt(DH)
    owners = (key_blocks // blk_dev).reshape(contexts, entries)
    within = (key_blocks % blk_dev).reshape(contexts, entries)
    is_live = (jnp.arange(KSLOTS)[None, :] < key_count[:, None]).reshape(contexts, entries)
    entry_ids = jnp.arange(entries)
    earlier = (
        (owners[:, :, None] == owners[:, None, :])
        & is_live[:, None, :]
        & (entry_ids[None, :] < entry_ids[:, None])[None]
    )
    rank_of = jnp.sum(earlier.astype(jnp.int32), axis=2)
    mine_owner = owners[position]
    mine_rank = rank_of[position]
    mine_live = is_live[position]
    kv_tiles = jnp.concatenate(
        [k_loc.reshape(blk_dev, tile_size), v_loc.reshape(blk_dev, tile_size)], axis=1
    )
    serve = (
        (is_live & (owners == position))[:, :, None, None]
        & (rank_of[:, :, None, None] == jnp.arange(slots_peer)[None, None, :, None])
        & (within[:, :, None, None] == jnp.arange(blk_dev)[None, None, None, :])
    )
    picker = jnp.any(serve, axis=1).reshape(contexts * slots_peer, blk_dev)
    outgoing = jnp.dot(
        picker.astype(jnp.bfloat16), kv_tiles, preferred_element_type=jnp.float32
    ).astype(jnp.bfloat16)
    incoming = lax.all_to_all(outgoing, "ctx", split_axis=0, concat_axis=0, tiled=True)
    target = mine_owner * slots_peer + mine_rank
    taker = (target[:, None] == jnp.arange(contexts * slots_peer)[None, :]) & mine_live[:, None]
    fetched = jnp.dot(
        taker.astype(jnp.bfloat16), incoming, preferred_element_type=jnp.float32
    ).astype(jnp.bfloat16)
    key_own = k_loc.reshape(blk_dev, 1, BLOCK, heads_loc, DH)
    value_own = v_loc.reshape(blk_dev, 1, BLOCK, heads_loc, DH)
    near_k = jnp.concatenate(
        [key_own, fetched[:, :tile_size].reshape(blk_dev, KSLOTS, BLOCK, heads_loc, DH)], axis=1
    ).reshape(blk_dev, key_width, heads_loc, DH)
    near_v = jnp.concatenate(
        [value_own, fetched[:, tile_size:].reshape(blk_dev, KSLOTS, BLOCK, heads_loc, DH)], axis=1
    ).reshape(blk_dev, key_width, heads_loc, DH)
    columns = jnp.repeat(
        jnp.concatenate(
            [jnp.ones((blk_dev, 1), dtype=bool), mine_live.reshape(blk_dev, KSLOTS)], axis=1
        ),
        BLOCK,
        axis=1,
    )
    q_tiles = q_loc.reshape(blk_dev, BLOCK, heads_loc, group_size, DH)
    o_tiles = o_loc.reshape(blk_dev, BLOCK, heads_loc, group_size, DH)

    def per_block(members):
        return attend(members[0], members[1], members[2], members[3], members[4], scaling)

    attended, grad_q, part_k, part_v = lax.map(
        per_block, (q_tiles, o_tiles, near_k, near_v, columns)
    )
    part_k = part_k.reshape(blk_dev, KSLOTS + 1, tile_size)
    part_v = part_v.reshape(blk_dev, KSLOTS + 1, tile_size)
    own_sums = jnp.concatenate([part_k[:, 0], part_v[:, 0]], axis=1)
    sent_terms = jnp.concatenate(
        [part_k[:, 1:].reshape(entries, tile_size), part_v[:, 1:].reshape(entries, tile_size)],
        axis=1,
    )
    outgoing_sums = jnp.dot(
        taker.astype(jnp.float32).T, sent_terms, precision=lax.Precision.HIGHEST
    )
    returned = lax.all_to_all(outgoing_sums, "ctx", split_axis=0, concat_axis=0, tiled=True)
    remote_sums = jnp.dot(picker.astype(jnp.float32).T, returned, precision=lax.Precision.HIGHEST)
    totals = own_sums + remote_sums
    grad_k = totals[:, :tile_size].astype(jnp.bfloat16).reshape(row_count, heads_loc * DH)
    grad_v = totals[:, tile_size:].astype(jnp.bfloat16).reshape(row_count, heads_loc * DH)
    attended = attended.reshape(row_count, heads_loc * group_size * DH)
    grad_q = grad_q.reshape(row_count, heads_loc * group_size * DH)
    return (attended, grad_q, grad_k, grad_v)


def solution(mesh):
    in_specs = (P("ctx", "head"), P("ctx", "head"), P("ctx", "head"), P("ctx", "head"), P(), P())
    out_specs = (P("ctx", "head"), P("ctx", "head"), P("ctx", "head"), P("ctx", "head"))
    return jax.shard_map(local, mesh=mesh, in_specs=in_specs, out_specs=out_specs, check_vma=False)
```

profile of v0, /device:TPU:0, one launch (start us, length us, event | category | flops | bytes accessed | tf_op | source)
XLA Modules:
  0.0 279.2 jit_solution(7897529669696669143)
XLA Ops:
  6.4 2.3 all_to_all.14
  8.7 7.4 %all-to-all-start = ((bf16[8,2,65536]{2,1,0:T(2,128)(2,1)}), bf16[8,2,65536]{2,1,0:T(2,128)(2,1)}, u32[]{:S(2)}, u32[]{:S(2)}) async-start(bf16[8,2,65536]{2,1,0:T(2,128)(2,1)} %all_to_all.14), calls=%async_computation | async-start | bytes 4194304 | tf_op jit(solution)/shard_map/all_to_all | solution.py:78
  19.2 45.3 %all-to-all-done = bf16[8,2,65536]{2,1,0:T(2,128)(2,1)} async-done(((bf16[8,2,65536]{2,1,0:T(2,128)(2,1)}), bf16[8,2,65536]{2,1,0:T(2,128)(2,1)}, u32[]{:S(2)}, u32[]{:S(2)}) %all-to-all-start) | async-done | bytes 2097184 | tf_op jit(solution)/shard_map/all_to_all | solution.py:78
  74.1 70.0 %while.16 = (s32[]{:T(128)}, bf16[2,128,2,8,128]{4,3,2,1,0:T(8,128)(2,1)}, bf16[2,128,2,8,128]{4,3,2,1,0:T(8,128)(2,1)}, f32[2,896,2,128]{3,2,1,0:T(2,128)}, f32...) while((s32[]{:T(128)}, ...), condition=%wide.region_6.7_spmd, body=%wide.region_2.6_spmd.sunk | while | flops 2842164224 | bytes 88649744 | solution.py:105
  77.0 7.0 %fusion.104 = (f32[2,8,128]{2,1,0:T(8,128)S(1)}, f32[2,8,128,896]{2,3,1,0:T(8,128)}) fusion(pred[896]{0:T(1024)(128)(4,1)S(1)} %dynamic-slice_reduce_fusion.2, bf16[1,128,2,8,128]{4,3,2,1,0:T(8,128)(2,1)S(1)} %constant_dynamic-slice_fusion.6, bf16[2,896,2,128]{3,1,2,0:T(8,128)(2,1)} %get-tuple-element.259, s32[]{:T(128)S(6)} %copy.231), kind=kOutput, calls=%fused_computation.98.clone.1 | convolution fusion | flops 478937984 | bytes 8333316 | tf_op jit(solution)/shard_map/while/body/eval_jaxpr/sub | solution.py:21
  84.0 4.1 %fusion.105 = bf16[2,8,128,896]{2,3,1,0:T(8,128)(2,1)S(1)} fusion(f32[2,8,128,896]{2,3,1,0:T(8,128)} %get-tuple-element.222, f32[2,8,128]{2,1,0:T(8,128)S(1)} %get-tuple-element.223), kind=kLoop, calls=%fused_computation.15.clone.1 | loop fusion | flops 3670016 | bytes 11018240 | tf_op jit(solution)/shard_map/while/body/eval_jaxpr/convert_element_type | solution.py:23
  91.1 6.7 %fusion.106 = bf16[2,8,128,896]{2,3,1,0:T(8,128)(2,1)} fusion(f32[2,8,128]{2,1,0:T(8,128)S(1)} %bitcast.189, f32[2,8,128,896]{2,3,1,0:T(8,128)} %get-tuple-element.222, f32[2,8,128]{2,1,0:T(8,128)S(1)} %get-tuple-element.223, bf16[1,128,2,8,128]{1,4,3,2,0:T(8,128)(2,1)S(1)} %copy.217, bf16[2,896,2,128]{3,1,2,0:T(8,128)(2,1)} %get-tuple-element.257, ...), kind=kOutput, calls=%fused_computation.4.clone.1 | convolution fusion | flops 478937088 | bytes 12009476 | tf_op jit(solution)/shard_map/while/body/eval_jaxpr/qhgd,khd->hgqk/dot_general | solution.py:28
  98.3 3.3 %convolution_bitcast_fusion.6 = f32[1,896,2,128]{1,3,2,0:T(8,128)S(1)} fusion(bf16[2,8,128,896]{2,3,1,0:T(8,128)(2,1)} %fusion.106, bf16[1,128,2,8,128]{4,3,2,1,0:T(8,128)(2,1)S(1)} %copy-done.2), kind=kOutput, calls=%fused_computation.17.clone.1 | convolution fusion | flops 469762048 | bytes 5111808 | tf_op jit(solution)/shard_map/while/body/eval_jaxpr/hgqk,qhgd->khd/dot_general | solution.py:35
  105.5 2.2 constant_dynamic-update-slice_fusion.6
  112.0 7.0 %fusion.104 = (f32[2,8,128]{2,1,0:T(8,128)S(1)}, f32[2,8,128,896]{2,3,1,0:T(8,128)}) fusion(pred[896]{0:T(1024)(128)(4,1)S(1)} %dynamic-slice_reduce_fusion.2, bf16[1,128,2,8,128]{4,3,2,1,0:T(8,128)(2,1)S(1)} %constant_dynamic-slice_fusion.6, bf16[2,896,2,128]{3,1,2,0:T(8,128)(2,1)} %get-tuple-element.259, s32[]{:T(128)S(6)} %copy.231), kind=kOutput, calls=%fused_computation.98.clone.1 | convolution fusion | flops 478937984 | bytes 8333316 | tf_op jit(solution)/shard_map/while/body/eval_jaxpr/sub | solution.py:21
  119.0 4.1 %fusion.105 = bf16[2,8,128,896]{2,3,1,0:T(8,128)(2,1)S(1)} fusion(f32[2,8,128,896]{2,3,1,0:T(8,128)} %get-tuple-element.222, f32[2,8,128]{2,1,0:T(8,128)S(1)} %get-tuple-element.223), kind=kLoop, calls=%fused_computation.15.clone.1 | loop fusion | flops 3670016 | bytes 11018240 | tf_op jit(solution)/shard_map/while/body/eval_jaxpr/convert_element_type | solution.py:23
  126.1 6.7 %fusion.106 = bf16[2,8,128,896]{2,3,1,0:T(8,128)(2,1)} fusion(f32[2,8,128]{2,1,0:T(8,128)S(1)} %bitcast.189, f32[2,8,128,896]{2,3,1,0:T(8,128)} %get-tuple-element.222, f32[2,8,128]{2,1,0:T(8,128)S(1)} %get-tuple-element.223, bf16[1,128,2,8,128]{1,4,3,2,0:T(8,128)(2,1)S(1)} %copy.217, bf16[2,896,2,128]{3,1,2,0:T(8,128)(2,1)} %get-tuple-element.257, ...), kind=kOutput, calls=%fused_computation.4.clone.1 | convolution fusion | flops 478937088 | bytes 12009476 | tf_op jit(solution)/shard_map/while/body/eval_jaxpr/qhgd,khd->hgqk/dot_general | solution.py:28
  133.3 3.3 %convolution_bitcast_fusion.6 = f32[1,896,2,128]{1,3,2,0:T(8,128)S(1)} fusion(bf16[2,8,128,896]{2,3,1,0:T(8,128)(2,1)} %fusion.106, bf16[1,128,2,8,128]{4,3,2,1,0:T(8,128)(2,1)S(1)} %copy-done.2), kind=kOutput, calls=%fused_computation.17.clone.1 | convolution fusion | flops 469762048 | bytes 5111808 | tf_op jit(solution)/shard_map/while/body/eval_jaxpr/hgqk,qhgd->khd/dot_general | solution.py:35
  144.1 3.0 %reshape.188 = f32[2,7,32768]{2,1,0:T(8,128)S(1)} reshape(f32[2,896,2,128]{3,2,1,0:T(2,128)} %get-tuple-element.62) | data formatting | bytes 3670016 | tf_op jit(solution)/shard_map/reshape | solution.py:109
  148.6 3.2 %reshape.190 = f32[12,32768]{1,0:T(8,128)} reshape(f32[2,6,32768]{2,1,0:T(8,128)} %slice.39) | data formatting | bytes 3145728 | tf_op jit(solution)/shard_map/reshape | solution.py:112
  151.8 4.3 %reshape.187 = f32[2,7,32768]{2,1,0:T(8,128)} reshape(f32[2,896,2,128]{3,2,1,0:T(2,128)} %get-tuple-element.61) | data formatting | bytes 3670016 | tf_op jit(solution)/shard_map/reshape | solution.py:108
  156.1 3.2 %slice.38 = f32[2,6,32768]{2,1,0:T(8,128)} slice(f32[2,7,32768]{2,1,0:T(8,128)} %reshape.187), slice={[0:2], [1:7], [0:32768]} | slice | bytes 3145728 | tf_op jit(solution)/shard_map/slice | solution.py:112
  159.3 3.1 %reshape.189 = f32[12,32768]{1,0:T(8,128)} reshape(f32[2,6,32768]{2,1,0:T(8,128)} %slice.38) | data formatting | bytes 3145728 | tf_op jit(solution)/shard_map/reshape | solution.py:112
  162.4 6.1 %fusion.46 = f32[16,65536]{1,0:T(8,128)} fusion(f32[12,32768]{1,0:T(8,128)} %reshape.190, f32[12,32768]{1,0:T(8,128)} %reshape.189, s32[12]{0:T(128)S(1)} %add_reduce_fusion, pred[12]{0:T(512)(128)(4,1)S(1)} %get-tuple-element.150), kind=kOutput, calls=%fused_computation.56 | convolution fusion | flops 151781760 | bytes 7340092 | tf_op jit(solution)/shard_map/dot_general | solution.py:115
  168.6 5.4 %all_to_all.17 = f32[8,2,65536]{2,1,0:T(2,128)} reshape(f32[16,65536]{1,0:T(8,128)} %fusion.46) | data formatting | bytes 8388608 | tf_op jit(solution)/shard_map/all_to_all | solution.py:118
  174.0 4.8 %all-to-all-start.1 = ((f32[8,2,65536]{2,1,0:T(2,128)}), f32[8,2,65536]{2,1,0:T(2,128)}, u32[]{:S(2)}, u32[]{:S(2)}) async-start(f32[8,2,65536]{2,1,0:T(2,128)} %all_to_all.17), calls=%async_computation.1 | async-start | bytes 8388608 | tf_op jit(solution)/shard_map/all_to_all | solution.py:118
  179.2 2.3 reshape.185
  183.0 88.1 %all-to-all-done.1 = f32[8,2,65536]{2,1,0:T(2,128)} async-done(((f32[8,2,65536]{2,1,0:T(2,128)}), f32[8,2,65536]{2,1,0:T(2,128)}, u32[]{:S(2)}, u32[]{:S(2)}) %all-to-all-start.1) | async-done | bytes 4194336 | tf_op jit(solution)/shard_map/all_to_all | solution.py:118
  271.1 6.4 %fusion.45 = bf16[2,65536]{1,0:T(2,128)(2,1)S(1)} fusion(pred[8,2,2]{0,2,1:T(4,128)(4,1)S(1)} %copy-done.10, f32[8,2,65536]{2,1,0:T(2,128)} %all-to-all-done.1, f32[2,32768]{1,0:T(2,128)S(1)} %bitcast.186, f32[2,32768]{1,0:T(2,128)S(1)} %bitcast.187), kind=kOutput, calls=%fused_computation.55 | convolution fusion | flops 25559040 | bytes 4980768 | tf_op jit(solution)/shard_map/dot_general | solution.py:119
  (115 shorter events, 48.8 us)
Async XLA Ops:
  2.6 0.6 copy-start.11
  3.5 1.2 copy-start.9
  6.4 9.8 %copy-start.7 = (bf16[256,256]{1,0:T(8,128)(2,1)S(1)}, bf16[256,256]{1,0:T(8,128)(2,1)}, u32[]{:S(2)}) copy-start(bf16[256,256]{1,0:T(8,128)(2,1)} %param.9) | copy-start | bytes 393220
  6.4 9.8 %copy-start.8 = (bf16[256,256]{1,0:T(8,128)(2,1)S(1)}, bf16[256,256]{1,0:T(8,128)(2,1)}, u32[]{:S(2)}) copy-start(bf16[256,256]{1,0:T(8,128)(2,1)} %param.10) | copy-start | bytes 393220
  6.4 10.2 %copy-start.4 = (bf16[256,2048]{1,0:T(8,128)(2,1)S(1)}, bf16[256,2048]{1,0:T(8,128)(2,1)}, u32[]{:S(2)}) copy-start(bf16[256,2048]{1,0:T(8,128)(2,1)} %param.8) | copy-start | bytes 3145732
  8.7 7.5 %copy-start.12 = (pred[8,12]{1,0:T(8,128)(4,1)S(1)}, pred[8,12]{1,0:T(8,128)(4,1)}, u32[]{:S(2)}) copy-start(pred[8,12]{1,0:T(8,128)(4,1)} %copy-done.11) | copy-start | bytes 292
  8.7 9.1 %copy-start.5 = (bf16[256,2048]{1,0:T(8,128)(2,1)S(1)}, bf16[256,2048]{1,0:T(8,128)(2,1)}, u32[]{:S(2)}) copy-start(bf16[256,2048]{1,0:T(8,128)(2,1)} %param.11) | copy-start | bytes 3145732
  8.7 55.8 %all-to-all-start = ((bf16[8,2,65536]{2,1,0:T(2,128)(2,1)}), bf16[8,2,65536]{2,1,0:T(2,128)(2,1)}, u32[]{:S(2)}, u32[]{:S(2)}) async-start(bf16[8,2,65536]{2,1,0:T(2,128)(2,1)} %all_to_all.14), calls=%async_computation | async-start | bytes 4194304 | tf_op jit(solution)/shard_map/all_to_all | solution.py:78
  75.2 8.8 %copy-start.1 = (bf16[1,128,2,8,128]{4,3,2,1,0:T(8,128)(2,1)}, bf16[1,128,2,8,128]{4,3,2,1,0:T(8,128)(2,1)S(1)}, u32[]{:S(2)}) copy-start(bf16[1,128,2,8,128]{4,3,2,1,0:T(8,128)(2,1)S(1)} %constant_dynamic-slice_fusion.6) | copy-start | bytes 1572868 | tf_op jit(solution)/shard_map/while
  84.0 4.1 %copy-start.3 = (bf16[2,896,2,128]{3,1,2,0:T(8,128)(2,1)S(1)}, bf16[2,896,2,128]{3,1,2,0:T(8,128)(2,1)}, u32[]{:S(2)}) copy-start(bf16[2,896,2,128]{3,1,2,0:T(8,128)(2,1)} %get-tuple-element.257) | copy-start | bytes 2752516 | tf_op jit(solution)/shard_map/while
  91.1 7.1 %copy-start.2 = (bf16[1,128,2,8,128]{4,3,2,1,0:T(8,128)(2,1)S(1)}, bf16[1,128,2,8,128]{4,3,2,1,0:T(8,128)(2,1)}, u32[]{:S(2)}) copy-start(bf16[1,128,2,8,128]{4,3,2,1,0:T(8,128)(2,1)} %copy-done.1) | copy-start | bytes 1572868 | tf_op jit(solution)/shard_map/while
  98.2 3.3 %copy-start = (bf16[2,8,128,896]{2,3,1,0:T(8,128)(2,1)S(1)}, bf16[2,8,128,896]{2,3,1,0:T(8,128)(2,1)}, u32[]{:S(2)}) copy-start(bf16[2,8,128,896]{2,3,1,0:T(8,128)(2,1)} %fusion.106) | copy-start | bytes 11010052 | tf_op jit(solution)/shard_map/while
  110.2 8.8 %copy-start.1 = (bf16[1,128,2,8,128]{4,3,2,1,0:T(8,128)(2,1)}, bf16[1,128,2,8,128]{4,3,2,1,0:T(8,128)(2,1)S(1)}, u32[]{:S(2)}) copy-start(bf16[1,128,2,8,128]{4,3,2,1,0:T(8,128)(2,1)S(1)} %constant_dynamic-slice_fusion.6) | copy-start | bytes 1572868 | tf_op jit(solution)/shard_map/while
  119.0 4.1 %copy-start.3 = (bf16[2,896,2,128]{3,1,2,0:T(8,128)(2,1)S(1)}, bf16[2,896,2,128]{3,1,2,0:T(8,128)(2,1)}, u32[]{:S(2)}) copy-start(bf16[2,896,2,128]{3,1,2,0:T(8,128)(2,1)} %get-tuple-element.257) | copy-start | bytes 2752516 | tf_op jit(solution)/shard_map/while
  126.1 7.1 %copy-start.2 = (bf16[1,128,2,8,128]{4,3,2,1,0:T(8,128)(2,1)S(1)}, bf16[1,128,2,8,128]{4,3,2,1,0:T(8,128)(2,1)}, u32[]{:S(2)}) copy-start(bf16[1,128,2,8,128]{4,3,2,1,0:T(8,128)(2,1)} %copy-done.1) | copy-start | bytes 1572868 | tf_op jit(solution)/shard_map/while
  133.3 3.3 %copy-start = (bf16[2,8,128,896]{2,3,1,0:T(8,128)(2,1)S(1)}, bf16[2,8,128,896]{2,3,1,0:T(8,128)(2,1)}, u32[]{:S(2)}) copy-start(bf16[2,8,128,896]{2,3,1,0:T(8,128)(2,1)} %fusion.106) | copy-start | bytes 11010052 | tf_op jit(solution)/shard_map/while
  174.0 97.1 %all-to-all-start.1 = ((f32[8,2,65536]{2,1,0:T(2,128)}), f32[8,2,65536]{2,1,0:T(2,128)}, u32[]{:S(2)}, u32[]{:S(2)}) async-start(f32[8,2,65536]{2,1,0:T(2,128)} %all_to_all.17), calls=%async_computation.1 | async-start | bytes 8388608 | tf_op jit(solution)/shard_map/all_to_all | solution.py:118
  178.8 2.7 copy-start.6
  178.8 4.0 %slice-start = ((f32[2,7,32768]{2,1,0:T(8,128)}), f32[2,1,32768]{2,1,0:T(1,128)S(1)}, s32[]{:S(2)}) async-start(f32[2,7,32768]{2,1,0:T(8,128)} %reshape.187), calls=%async_computation.2 | async-start | bytes 524288 | tf_op jit(solution)/shard_map/slice | solution.py:110
  178.8 92.3 %copy-start.10 = (pred[8,2,2]{0,2,1:T(4,128)(4,1)S(1)}, pred[8,2,2]{0,2,1:T(4,128)(4,1)}, u32[]{:S(2)}) copy-start(pred[8,2,2]{0,2,1:T(4,128)(4,1)} %copy-done.9) | copy-start | bytes 100
where the time goes:
time: 280 us; the launch traced here: 279 us
  waiting for transfers between devices  133 us (48%)
  local copies, waits for them, and re-layouts  64.8 us (23%)
  matrix products  55.9 us (20%)
  starting transfers between devices  12.2 us (4%)
  other arithmetic  11.7 us (4%)
    all_to_all x1, waiting for transfers between devices, local(): lax.all_to_all(outgoing_sums, 'ctx', split_axis=0, concat_axis=0, tiled=T...  88.1 us
    all_to_all x1, waiting for transfers between devices, local(): lax.all_to_all(outgoing, 'ctx', split_axis=0, concat_axis=0, tiled=True)  45.3 us
    dynamic_update_slice x12, local copies, waits for them, and re-layouts, local(): lax.map(per_block, (q_tiles, o_tiles, near_k, near_v, columns))  14.2 us
    sub x2, matrix products, attend(): expo_terms = jnp.where(column, jnp.exp(scores - row_max), 0.0)  14.1 us
    dot_general x2, matrix products, attend(): jnp.einsum('qhgd,khd->hgqk', o_blk, near_v, preferred_element_type=jnp.fl...  13.3 us
    convert_element_type x2, other arithmetic, attend(): weights = prob_rows.astype(jnp.bfloat16)  8.1 us
    all_to_all x1, starting transfers between devices, local(): lax.all_to_all(outgoing, 'ctx', split_axis=0, concat_axis=0, tiled=True)  7.41 us
    dot_general x2, matrix products, attend(): jnp.einsum('hgqk,qhgd->khd', grad_s, q_blk, preferred_element_type=jnp.fl...  6.64 us
  transfers between devices with their start and end apart: 2, of which 2 were waited for; matrix products, arithmetic and copies ran while one was open for 3% of the time, Pallas kernels for 0%

commit v1 on v0

v1 whole, which is shorter than its diff:
```python
import functools
import math

import jax
import jax.numpy as jnp
from jax import lax
from jax.experimental import pallas as pl
from jax.experimental.pallas import tpu as pltpu
from jax.sharding import PartitionSpec as P


QH = 64
KVH = 8
DH = 128
BLOCK = 128

SCALE = 1.0 / math.sqrt(DH)
EXP2_SCALE = SCALE * math.log2(math.e)
FIRST_TILE = 512
NEAR_TILE = 512
TURN_TILE = 512
BACK_TILE = 512
NEAR_UNROLL = 1
TURN_UNROLL = 1
BACK_UNROLL = 1
VMEM_BYTES = 24 * 1024 * 1024

NT = (((1,), (1,)), ((), ()))
VMEM = pl.BlockSpec(memory_space=pltpu.VMEM)
SMEM = pl.BlockSpec(memory_space=pltpu.SMEM)
HBM = pl.BlockSpec(memory_space=pltpu.HBM)


def dot(a, b):
    return jnp.dot(a, b, preferred_element_type=jnp.float32)


def dot_t(a, b):
    return lax.dot_general(a, b, NT, preferred_element_type=jnp.float32)


def bf16(shape):
    return jax.ShapeDtypeStruct(shape, jnp.bfloat16)


def f32(shape):
    return jax.ShapeDtypeStruct(shape, jnp.float32)


def call(kernel, in_specs, out_shape, flops, args, scratch=(), out_specs=None):
    return pl.pallas_call(
        kernel,
        in_specs=in_specs,
        out_specs=out_specs or [VMEM] * len(out_shape),
        out_shape=out_shape,
        scratch_shapes=list(scratch),
        compiler_params=pltpu.CompilerParams(vmem_limit_bytes=VMEM_BYTES),
        cost_estimate=pl.CostEstimate(
            flops=int(flops), bytes_accessed=1 << 20, transcendentals=0
        ),
    )(*args)


def at(index, size):
    return pl.ds(pl.multiple_of(index * size, size), size)


def slot(w):
    return jnp.maximum(w, 0)


def block_of(ref, w, h, base=0):
    start = pl.multiple_of(base + slot(w) * BLOCK, BLOCK)
    return ref[pl.ds(start, BLOCK), at(h, DH)]


def key_of(ref, w, h, own):
    return jnp.where(w >= 0, block_of(ref, w, h), own)


def keep(w, x):
    return jnp.where(w >= 0, x, jnp.zeros_like(x))


def value_and_one(v, w):
    return keep(w, jnp.concatenate([v, jnp.ones_like(v)], axis=1))


def rows_of(*blocks):
    return jnp.concatenate(blocks, axis=0)


def tiles(rows, size):
    return [slice(t, t + size) for t in range(0, rows, size)]


def copies_of(src, dst, sems):
    copies = [pltpu.make_async_copy(s, d, sems.at[i]) for i, (s, d) in enumerate(zip(src, dst))]
    for c in copies:
        c.start()
    return copies


def pack_kernel(k_ref, v_ref, kv_ref, sems):
    rows = k_ref.shape[0]
    halves = [kv_ref.at[pl.ds(0, rows)], kv_ref.at[pl.ds(rows, rows)]]
    for c in copies_of([k_ref, v_ref], halves, sems):
        c.wait()


def first_kernel(heads, q_in, o_in, kv_ref, q_ref, o_ref, qt_ref, ot_ref, acc_ref, m_ref, sems):
    combos, rows, _ = q_ref.shape
    group = rows // BLOCK
    half = kv_ref.shape[0] // 2
    for c in range(combos):
        b, h = c // heads, c % heads
        for g in range(group):
            src = (pl.ds(b * BLOCK, BLOCK), pl.ds((h * group + g) * DH, DH))
            dst = pl.ds(g * BLOCK, BLOCK)
            pltpu.make_async_copy(q_in.at[src], q_ref.at[c, dst], sems.at[0, c]).start()
            pltpu.make_async_copy(o_in.at[src], o_ref.at[c, dst], sems.at[1, c]).start()

    def combo(c, carry):
        b, h = c // heads, c % heads
        pltpu.make_async_copy(q_ref.at[c], q_ref.at[c], sems.at[0, c]).wait()
        k = block_of(kv_ref, b, h)
        v = value_and_one(block_of(kv_ref, b, h, half), 0)
        for part in tiles(rows, FIRST_TILE):
            x = dot_t(q_ref[c, part, :], k) * EXP2_SCALE
            m = jnp.max(x, axis=1, keepdims=True)
            p = jnp.exp2(x - m)
            m_ref[c, part, :] = jnp.broadcast_to(m, x.shape)
            acc_ref[c, part, :] = dot(p.astype(jnp.bfloat16), v)
        pltpu.make_async_copy(o_ref.at[c], o_ref.at[c], sems.at[1, c]).wait()
        for src, dst in ((q_ref, qt_ref), (o_ref, ot_ref)):
            for part in tiles(rows, BLOCK):
                dst[c, :, part] = src[c, part, :].T
        return carry

    lax.fori_loop(0, combos, combo, 0)


def first(q, o, kv, combos, heads, group):
    rows = group * BLOCK
    return call(
        functools.partial(first_kernel, heads),
        [HBM] * 2 + [VMEM],
        [bf16((combos, rows, DH))] * 2
        + [bf16((combos, DH, rows))] * 2
        + [f32((combos, rows, 2 * DH)), f32((combos, rows, DH))],
        6 * combos * rows * BLOCK * DH,
        (q, o, kv),
        [pltpu.SemaphoreType.DMA((2, combos))],
    )


def near_kernel(
    heads, ja, jb, tbl, q_ref, kv_ref, a_ref, b_ref, acc_in, m_in, acc_ref, m_ref
):
    combos, rows, _ = q_ref.shape
    half = a_ref.shape[0] // 2

    def combo(c, carry):
        b, h = c // heads, c % heads
        wa, wb = tbl[b, ja], tbl[b, jb]
        own = block_of(kv_ref, b, h)
        k = rows_of(key_of(a_ref, wa, h, own), key_of(b_ref, wb, h, own))
        v = rows_of(
            value_and_one(block_of(a_ref, wa, h, half), wa),
            value_and_one(block_of(b_ref, wb, h, half), wb),
        )
        for part in tiles(rows, NEAR_TILE):
            x = dot_t(q_ref[c, part, :], k) * EXP2_SCALE
            old = m_in[c, part, :]
            m = jnp.maximum(old, jnp.max(x, axis=1, keepdims=True))
            a = jnp.exp2(old - m)
            p = jnp.exp2(x - jnp.concatenate([m, m], axis=1))
            m_ref[c, part, :] = m
            acc = acc_in[c, part, :] * jnp.concatenate([a, a], axis=1)
            acc_ref[c, part, :] = acc + dot(p.astype(jnp.bfloat16), v)
        return carry

    lax.fori_loop(0, combos, combo, 0, unroll=NEAR_UNROLL)


def near(tbl, q, kv, a, b, state, ja, jb, heads):
    combos, rows, _ = q.shape
    return call(
        functools.partial(near_kernel, heads, ja, jb),
        [SMEM] + [VMEM] * 6,
        [f32((combos, rows, 2 * DH)), f32((combos, rows, DH))],
        8 * combos * rows * BLOCK * DH,
        (tbl, q, kv, a, b, *state),
    )


def turn_kernel(
    heads, opposite, tbl, q_ref, o_ref, qt_ref, ot_ref, kv_ref, k_ref, v_ref, acc_in, m_in,
    att_ref, lse_ref, delta_ref, ds_ref, pk_ref, pv_ref, w_scr, pk_scr, pv_scr,
):
    combos, rows, _ = q_ref.shape
    pk_scr[...] = jnp.zeros_like(pk_scr)
    pv_scr[...] = jnp.zeros_like(pv_scr)

    def combo(c, carry):
        b, h = c // heads, c % heads
        w = tbl[b, opposite]
        k4 = key_of(k_ref, w, h, block_of(kv_ref, b, h))
        v4 = block_of(v_ref, w, h)
        v_one = value_and_one(v4, w)
        for part in tiles(rows, TURN_TILE):
            x = dot_t(q_ref[c, part, :], k4) * EXP2_SCALE
            grad_p = dot_t(o_ref[c, part, :], v4)
            old = m_in[c, part, :]
            m = jnp.maximum(old, jnp.max(x, axis=1, keepdims=True))
            a = jnp.exp2(old - m)
            p = jnp.exp2(x - m)
            acc = acc_in[c, part, :] * jnp.concatenate([a, a], axis=1)
            acc = acc + dot(p.astype(jnp.bfloat16), v_one)
            total = acc[:, DH:]
            inverse = 1.0 / total
            att = (acc[:, :DH] * inverse).astype(jnp.bfloat16)
            att_ref[c, part, :] = att
            delta = jnp.sum(
                o_ref[c, part, :].astype(jnp.float32) * att.astype(jnp.float32),
                axis=1,
                keepdims=True,
            )
            p = p * inverse
            w_scr[part, :] = p.astype(jnp.bfloat16)
            ds_ref[c, part, :] = (p * (grad_p - delta)).astype(jnp.bfloat16)
            lse_ref[c, part, :] = m + jnp.log2(total)
            delta_ref[c, part, :] = jnp.broadcast_to(delta, x.shape)
        pk_scr[at(h, DH), at(slot(w), BLOCK)] += keep(w, dot(qt_ref[c], ds_ref[c]))
        pv_scr[at(h, DH), at(slot(w), BLOCK)] += keep(w, dot(ot_ref[c], w_scr[...]))
        return carry

    lax.fori_loop(0, combos, combo, 0, unroll=TURN_UNROLL)
    pk_ref[...] = pk_scr[...].astype(jnp.bfloat16)
    pv_ref[...] = pv_scr[...].astype(jnp.bfloat16)


def turn(tbl, slabs, kv, k4, v4, state, opposite, heads):
    combos, rows, _ = slabs[0].shape
    own_rows = k4.shape[0]
    shape = (combos, rows, DH)
    return call(
        functools.partial(turn_kernel, heads, opposite),
        [SMEM] + [VMEM] * 9,
        [bf16(shape), f32(shape), f32(shape), bf16(shape)] + [bf16((heads * DH, own_rows))] * 2,
        10 * combos * rows * BLOCK * DH,
        (tbl, *slabs, kv, k4, v4, *state),
        [pltpu.VMEM((rows, DH), jnp.bfloat16)]
        + [pltpu.VMEM((heads * DH, own_rows), jnp.float32)] * 2,
    )


def weights_and_grads(c, q_ref, o_ref, lse_ref, delta_ref, k, v, ds_scr, w_scr):
    repeat = k.shape[0] // BLOCK
    for part in tiles(q_ref.shape[1], BACK_TILE):
        lse = jnp.concatenate([lse_ref[c, part, :]] * repeat, axis=1)
        delta = jnp.concatenate([delta_ref[c, part, :]] * repeat, axis=1)
        p = jnp.exp2(dot_t(q_ref[c, part, :], k) * EXP2_SCALE - lse)
        w_scr[part, :] = p.astype(jnp.bfloat16)
        ds_scr[part, :] = (p * (dot_t(o_ref[c, part, :], v) - delta)).astype(jnp.bfloat16)


def back_kernel(
    heads, ja, jb, has_sum, tbl, q_ref, o_ref, qt_ref, ot_ref, kv_ref, lse_ref, delta_ref, a_ref,
    b_ref, *refs,
):
    if has_sum:
        gq_in, *refs = refs
    pa_ref, pb_ref, gq_ref, ds_scr, w_scr = refs
    combos, rows, _ = q_ref.shape
    half = a_ref.shape[0] // 2
    pa_ref[...] = jnp.zeros_like(pa_ref)
    pb_ref[...] = jnp.zeros_like(pb_ref)

    def combo(c, carry):
        b, h = c // heads, c % heads
        wa, wb = tbl[b, ja], tbl[b, jb]
        own = block_of(kv_ref, b, h)
        ka, kb = key_of(a_ref, wa, h, own), key_of(b_ref, wb, h, own)
        v = rows_of(block_of(a_ref, wa, h, half), block_of(b_ref, wb, h, half))
        weights_and_grads(
            c, q_ref, o_ref, lse_ref, delta_ref, rows_of(ka, kb), v, ds_scr, w_scr
        )
        dk = dot(qt_ref[c], ds_scr[...])
        dv = dot(ot_ref[c], w_scr[...])
        for i, (ref, w) in enumerate(((pa_ref, wa), (pb_ref, wb))):
            src = slice(i * BLOCK, (i + 1) * BLOCK)
            ref[at(h, DH), at(slot(w), BLOCK)] += keep(w, dk[:, src])
            ref[at(heads + h, DH), at(slot(w), BLOCK)] += keep(w, dv[:, src])
        used = rows_of(keep(wa, ka), keep(wb, kb))
        for part in tiles(rows, BACK_TILE):
            grad = dot(ds_scr[part, :], used)
            gq_ref[c, part, :] = gq_in[c, part, :] + grad if has_sum else grad
        return carry

    lax.fori_loop(0, combos, combo, 0, unroll=BACK_UNROLL)


def back(tbl, slabs, kv, stats, a, b, gq, ja, jb, heads):
    combos, rows, _ = slabs[0].shape
    own_rows = a.shape[0] // 2
    extra = () if gq is None else (gq,)
    return call(
        functools.partial(back_kernel, heads, ja, jb, gq is not None),
        [SMEM] + [VMEM] * (9 + len(extra)),
        [f32((2 * heads * DH, own_rows))] * 2 + [f32((combos, rows, DH))],
        20 * combos * rows * BLOCK * DH,
        (tbl, *slabs, kv, *stats, a, b, *extra),
        [pltpu.VMEM((rows, 2 * BLOCK), jnp.bfloat16)] * 2,
    )


def own_kernel(
    heads, opposite, tbl, q_ref, o_ref, qt_ref, ot_ref, kv_ref, lse_ref, delta_ref, k4_ref,
    ds4_ref, att_ref, gq_in, att_out, gq_out, part_ref, ds_scr, w_scr, gq_scr, sems,
):
    combos, rows, _ = q_ref.shape
    group = rows // BLOCK
    half = kv_ref.shape[0] // 2

    def sends(ref, out, c, sem):
        b, h = c // heads, c % heads
        return [
            pltpu.make_async_copy(
                ref.at[c, pl.ds(g * BLOCK, BLOCK)],
                out.at[at(b, BLOCK), at(h * group + g, DH)],
                sem,
            )
            for g in range(group)
        ]

    def combo(c, carry):
        b, h = c // heads, c % heads
        for send in sends(att_ref, att_out, c, sems.at[0, c]):
            send.start()
        k, v = block_of(kv_ref, b, h), block_of(kv_ref, b, h, half)
        weights_and_grads(c, q_ref, o_ref, lse_ref, delta_ref, k, v, ds_scr, w_scr)
        part_ref[at(h, DH), at(b, BLOCK)] = dot(qt_ref[c], ds_scr[...])
        part_ref[at(heads + h, DH), at(b, BLOCK)] = dot(ot_ref[c], w_scr[...])
        w4 = tbl[b, opposite]
        used = rows_of(k, keep(w4, block_of(k4_ref, w4, h)))
        for part in tiles(rows, BACK_TILE):
            ds = jnp.concatenate([ds_scr[part, :], ds4_ref[c, part, :]], axis=1)
            grad = (gq_in[c, part, :] + dot(ds, used)) * SCALE
            gq_scr[c, part, :] = grad.astype(jnp.bfloat16)
        for send in sends(gq_scr, gq_out, c, sems.at[1, c]):
            send.start()
        return carry

    lax.fori_loop(0, combos, combo, 0)
    for c in range(combos):
        pltpu.make_async_copy(att_ref.at[c], att_ref.at[c], sems.at[0, c]).wait()
        pltpu.make_async_copy(gq_scr.at[c], gq_scr.at[c], sems.at[1, c]).wait()


def own(tbl, slabs, kv, stats, k4, ds4, att, gq, opposite, heads, q_shape):
    combos, rows, _ = slabs[0].shape
    return call(
        functools.partial(own_kernel, heads, opposite),
        [SMEM] + [VMEM] * 11,
        [bf16(q_shape), bf16(q_shape), f32((2 * heads * DH, kv.shape[0] // 2))],
        12 * combos * rows * BLOCK * DH,
        (tbl, *slabs, kv, *stats, k4, ds4, att, gq),
        [pltpu.VMEM((rows, BLOCK), jnp.bfloat16)] * 2
        + [pltpu.VMEM((combos, rows, DH), jnp.bfloat16), pltpu.SemaphoreType.DMA((2, combos))],
        [HBM, HBM, VMEM],
    )


def finish_kernel(own_ref, a_ref, b_ref, gk_ref, gv_ref):
    total = own_ref[...] + (a_ref[...].astype(jnp.float32) + b_ref[...].astype(jnp.float32))
    half = total.shape[0] // 2
    gk_ref[...] = (total[:half, :] * SCALE).T.astype(jnp.bfloat16)
    gv_ref[...] = total[half:, :].T.astype(jnp.bfloat16)


def local(queries, keys, values, grad_out, key_blocks, key_count):
    n = lax.axis_size("ctx")
    me = lax.axis_index("ctx")
    row_count, width = keys.shape
    blk_dev = row_count // BLOCK
    heads = width // DH
    group = QH // KVH
    combos = blk_dev * heads
    opposite = n // 2
    steps = opposite - 1

    order = list(range(0, n, 2)) + list(range(n - 1, 0, -2))
    up = [(order[i], order[(i + 1) % n]) for i in range(n)]
    down = [(b, a) for a, b in up]

    def place(index):
        return jnp.where(index % 2 == 0, index // 2, n - 1 - index // 2)

    def hop(x, perm):
        return lax.ppermute(x, "ctx", perm)

    kv = call(
        pack_kernel, [HBM] * 2, [bf16((2 * row_count, width))], 1e6, (keys, values),
        [pltpu.SemaphoreType.DMA((2,))],
    )[0]

    blocks = lax.dynamic_slice_in_dim(key_blocks, me * blk_dev, blk_dev, 0)
    counts = lax.dynamic_slice_in_dim(key_count, me * blk_dev, blk_dev, 0)
    live = jnp.arange(blocks.shape[1])[None, :] < counts[:, None]
    offset = (place(blocks // blk_dev) - place(me) + n) % n
    hit = live[:, :, None] & (offset[:, :, None] == jnp.arange(n)[None, None, :])
    tbl = jnp.sum(jnp.where(hit, (blocks % blk_dev)[:, :, None] + 1, 0), axis=1) - 1

    q, o, qt, ot, *state = first(queries, grad_out, kv, combos, heads, group)
    slabs = (q, o, qt, ot)
    behind, ahead = [kv], [kv]
    for s in range(1, steps + 1):
        behind.append(hop(behind[-1], up))
        ahead.append(hop(ahead[-1], down))
        state = near(tbl, q, kv, ahead[s], behind[s], state, s, n - s, heads)
    k4 = hop(behind[-1][:row_count], up)
    v4 = hop(ahead[-1][row_count:], down)

    att, lse, delta, ds4, pk, pv = turn(tbl, slabs, kv, k4, v4, state, opposite, heads)
    stats = (lse, delta)

    up_in = hop(pk, up)
    down_in = hop(pv, down)
    half = heads * DH
    gq = None
    for s in range(steps, 0, -1):
        part_a, part_b, gq = back(tbl, slabs, kv, stats, ahead[s], behind[s], gq, s, n - s, heads)
        if s == steps:
            up_out = jnp.concatenate([part_a[:half] + up_in.astype(jnp.float32), part_a[half:]])
            down_out = jnp.concatenate([part_b[:half], part_b[half:] + down_in.astype(jnp.float32)])
        else:
            up_out = part_a + up_in.astype(jnp.float32)
            down_out = part_b + down_in.astype(jnp.float32)
        up_in = hop(up_out.astype(jnp.bfloat16), up)
        down_in = hop(down_out.astype(jnp.bfloat16), down)
    attended, grad_q, own_part = own(
        tbl, slabs, kv, stats, k4, ds4, att, gq, opposite, heads, queries.shape
    )
    grad_k, grad_v = call(
        finish_kernel, [VMEM] * 3, [bf16(keys.shape)] * 2, 1e7,
        (own_part, up_in, down_in),
    )
    return attended, grad_q, grad_k, grad_v


def solution(mesh):
    spec = P("ctx", "head")
    return jax.shard_map(
        local,
        mesh=mesh,
        in_specs=(spec, spec, spec, spec, P(), P()),
        out_specs=(spec,) * 4,
        check_vma=False,
    )
```

time: 280 us -> 78.3 us (0.28)
  waiting for transfers between devices: 133 us -> 15.8 us
  local copies, waits for them, and re-layouts: 64.8 us -> 5.02 us
  matrix products: 55.9 us -> 0 us
  Pallas kernels: 0 us -> 36 us
  other arithmetic: 11.7 us -> 2.01 us
  starting transfers between devices: 12.2 us -> 18.3 us
    all_to_all x2 -> x0, waiting for transfers between devices: 133 us -> none  [the longest x1 88.1 us: local(): lax.all_to_all(outgoing_sums, 'ctx', split_axis=0, concat_axis=0, tiled=T...]
    dot_general x14 -> x0, matrix products: 41.8 us -> none  [the longest x2 13.3 us: attend(): jnp.einsum('qhgd,khd->hgqk', o_blk, near_v, preferred_element_type=jnp.fl...]
    pallas_call x0 -> x11, Pallas kernels: none -> 36 us  [call(): pl.pallas_call(kernel, in_specs=in_specs, out_specs=out_specs or [VMEM] *...]
    reshape x19 -> x0, local copies, waits for them, and re-layouts: 24.1 us -> none  [the longest x1 4.32 us: local(): part_k = part_k.reshape(blk_dev, KSLOTS + 1, tile_size)]
    ppermute x0 -> x16, starting transfers between devices: none -> 18.3 us  [hop(): return lax.ppermute(x, 'ctx', perm)]
    ppermute x0 -> x16, waiting for transfers between devices: none -> 15.8 us  [hop(): return lax.ppermute(x, 'ctx', perm)]
    dynamic_update_slice x12 -> x0, local copies, waits for them, and re-layouts: 14.2 us -> none  [local(): lax.map(per_block, (q_tiles, o_tiles, near_k, near_v, columns))]
    sub x2 -> x0, matrix products: 14.1 us -> none  [attend(): expo_terms = jnp.where(column, jnp.exp(scores - row_max), 0.0)]
  transfers between devices with their start and end apart: 2 -> 16, of which waited for: 2 -> 6; matrix products, arithmetic and copies ran while one was open for 3% -> 4% of each run, Pallas kernels for 0% -> 38%
where the time goes in v1:
time: 78.3 us; the launch traced here: 78 us
  Pallas kernels  36 us (46%)
  starting transfers between devices  18.3 us (23%)
  waiting for transfers between devices  15.8 us (20%)
  local copies, waits for them, and re-layouts  5.02 us (6%)
  other arithmetic  2.01 us (3%)
  between operations  0.85 us (1%)
    pallas_call x11, Pallas kernels, call(): pl.pallas_call(kernel, in_specs=in_specs, out_specs=out_specs or [VMEM] *...  36 us
    ppermute x16, starting transfers between devices, hop(): return lax.ppermute(x, 'ctx', perm)  18.3 us
    ppermute x16, waiting for transfers between devices, hop(): return lax.ppermute(x, 'ctx', perm)  15.8 us
    unnamed x8, local copies, waits for them, and re-layouts  4.25 us
  transfers between devices with their start and end apart: 16, of which 6 were waited for; matrix products, arithmetic and copies ran while one was open for 4% of the time, Pallas kernels for 38%

profile of v1, /device:TPU:0, one launch (start us, length us, event | category | flops | bytes accessed | tf_op | source)
XLA Modules:
  0.0 78.0 jit_solution(2567240646637539489)
XLA Ops:
  2.8 3.0 %collective-permute-start.4 = (bf16[512,256]{1,0:T(8,128)(2,1)S(1)}, bf16[512,256]{1,0:T(8,128)(2,1)S(1)}, u32[]{:S(2)}, u32[]{:S(2)}) collective-permute-start(bf16[512,256]{1,0:T(8,128)(2,1)S(1)} %shard_map.93.kv_ref), channel_id=1, source_target_pairs={{8,0},{16,8},{24,16},{28,24},{20,28},{12,20},{4,12},{0,4},{9,1},{1... | collective-permute-start | bytes 786440 | tf_op jit(solution)/shard_map/ppermute | solution.py:401
  6.7 5.5 %collective-permute-done.4.a_ref = bf16[512,256]{1,0:T(8,128)(2,1)S(1)} collective-permute-done((bf16[512,256]{1,0:T(8,128)(2,1)S(1)}, bf16[512,256]{1,0:T(8,128)(2,1)S(1)}, u32[]{:S(2)}, u32[]{:S(2)}) %collective-permute-start.4) | collective-permute-done | bytes 262176 | tf_op jit(solution)/shard_map/ppermute | solution.py:401
  12.2 1.7 %collective-permute-start.5 = (bf16[512,256]{1,0:T(8,128)(2,1)S(1)}, bf16[512,256]{1,0:T(8,128)(2,1)S(1)}, u32[]{:S(2)}, u32[]{:S(2)}) collective-permute-start(bf16[512,256]{1,0:T(8,128)(2,1)S(1)} %collective-permute-done.4.a_ref), channel_id=1, source_target_pairs={{8,0},{16,8},{24,16},{28,24},{20,28},{12,20},{4,12},{0,4},{9,1},{1... | collective-permute-start | bytes 786440 | tf_op jit(solution)/shard_map/ppermute | solution.py:401
  15.8 3.9 %collective-permute-done.5.a_ref = bf16[512,256]{1,0:T(8,128)(2,1)S(1)} collective-permute-done((bf16[512,256]{1,0:T(8,128)(2,1)S(1)}, bf16[512,256]{1,0:T(8,128)(2,1)S(1)}, u32[]{:S(2)}, u32[]{:S(2)}) %collective-permute-start.5) | collective-permute-done | bytes 262176 | tf_op jit(solution)/shard_map/ppermute | solution.py:401
  19.7 1.4 %collective-permute-start.6 = (bf16[512,256]{1,0:T(8,128)(2,1)S(1)}, bf16[512,256]{1,0:T(8,128)(2,1)S(1)}, u32[]{:S(2)}, u32[]{:S(2)}) collective-permute-start(bf16[512,256]{1,0:T(8,128)(2,1)S(1)} %collective-permute-done.5.a_ref), channel_id=1, source_target_pairs={{8,0},{16,8},{24,16},{28,24},{20,28},{12,20},{4,12},{0,4},{9,1},{1... | collective-permute-start | bytes 786440 | tf_op jit(solution)/shard_map/ppermute | solution.py:401
  21.8 1.2 %copy-done = bf16[256,2048]{1,0:T(8,128)(2,1)S(1)} copy-done((bf16[256,2048]{1,0:T(8,128)(2,1)S(1)}, bf16[256,2048]{1,0:T(8,128)(2,1)}, u32[]{:S(2)}) %copy-start) | copy-done | bytes 1048600
  23.0 1.2 %copy-done.1 = bf16[256,2048]{1,0:T(8,128)(2,1)S(1)} copy-done((bf16[256,2048]{1,0:T(8,128)(2,1)S(1)}, bf16[256,2048]{1,0:T(8,128)(2,1)}, u32[]{:S(2)}) %copy-start.1) | copy-done | bytes 1048600
  24.2 4.4 %shard_map.94 = (bf16[4,1024,128]{2,1,0:T(8,128)(2,1)S(1)}, bf16[4,1024,128]{2,1,0:T(8,128)(2,1)S(1)}, bf16[4,128,1024]{2,1,0:T(8,128)(2,1)S(1)}, bf16[4,128,102...) custom-call(bf16[256,2048]{1,0:T(8,128)(2,1)S(1)} %copy-done, ...), custom_call_target="tpu_custom_call" | custom-call | flops 402653184 | bytes 1048576 | tf_op jit(solution)/shard_map/pallas_call | solution.py:51
  28.7 1.4 %collective-permute-start.7 = (bf16[256,256]{1,0:T(8,128)(2,1)S(1)}, bf16[256,256]{1,0:T(8,128)(2,1)S(1)}, u32[]{:S(2)}, u32[]{:S(2)}) collective-permute-start(bf16[256,256]{1,0:T(8,128)(2,1)S(1)} %slice.27), channel_id=1, source_target_pairs={{8,0},{16,8},{24,16},{28,24},{20,28},{12,20},{4,12},{0,4},{9,1},{1... | collective-permute-start | bytes 393224 | tf_op jit(solution)/shard_map/ppermute | solution.py:401
  30.9 3.2 %shard_map.95 = (f32[4,1024,256]{2,1,0:T(8,128)S(1)}, f32[4,1024,128]{2,1,0:T(8,128)S(1)}) custom-call(s32[2,8]{1,0:T(2,128)S(1)} %broadcast_add_fusion.tbl, bf16[4,1024,128]{2,1,0:T(8,128)(2,1)S(1)} %get-tuple-element.36.q_ref, bf16[512,256]{1,0:T(8,128)(2,1)S(1)} %shard_map.93.kv_ref, bf16[512,256]{1,0:T(8,128)(2,1)S(1)} %collective-permute-done.4.a_ref, ...), custom_call_target="tpu_custom_call" | custom-call | flops 536870912 | bytes 1048576 | tf_op jit(solution)/shard_map/pallas_call | solution.py:51
  34.1 3.2 %shard_map.96 = (f32[4,1024,256]{2,1,0:T(8,128)S(1)}, f32[4,1024,128]{2,1,0:T(8,128)S(1)}) custom-call(s32[2,8]{1,0:T(2,128)S(1)} %broadcast_add_fusion.tbl, bf16[4,1024,128]{2,1,0:T(8,128)(2,1)S(1)} %get-tuple-element.36.q_ref, bf16[512,256]{1,0:T(8,128)(2,1)S(1)} %shard_map.93.kv_ref, bf16[512,256]{1,0:T(8,128)(2,1)S(1)} %collective-permute-done.5.a_ref, ...), custom_call_target="tpu_custom_call" | custom-call | flops 536870912 | bytes 1048576 | tf_op jit(solution)/shard_map/pallas_call | solution.py:51
  37.3 3.2 %shard_map.97 = (f32[4,1024,256]{2,1,0:T(8,128)S(1)}, f32[4,1024,128]{2,1,0:T(8,128)S(1)}) custom-call(s32[2,8]{1,0:T(2,128)S(1)} %broadcast_add_fusion.tbl, bf16[4,1024,128]{2,1,0:T(8,128)(2,1)S(1)} %get-tuple-element.36.q_ref, bf16[512,256]{1,0:T(8,128)(2,1)S(1)} %shard_map.93.kv_ref, bf16[512,256]{1,0:T(8,128)(2,1)S(1)} %collective-permute-done.6.a_ref, ...), custom_call_target="tpu_custom_call" | custom-call | flops 536870912 | bytes 1048576 | tf_op jit(solution)/shard_map/pallas_call | solution.py:51
  40.6 5.1 %shard_map.98 = (bf16[4,1024,128]{2,1,0:T(8,128)(2,1)S(1)}, f32[4,1024,128]{2,1,0:T(8,128)S(1)}, f32[4,1024,128]{2,1,0:T(8,128)S(1)}, bf16[4,1024,128]{2,1,0:T(8...) custom-call(s32[2,8]{1,0:T(2,128)S(1)} %broadcast_add_fusion.tbl, ...), custom_call_target="tpu_custom_call" | custom-call | flops 671088640 | bytes 1048576 | tf_op jit(solution)/shard_map/pallas_call | solution.py:51
  45.7 1.5 %collective-permute-start.8 = (bf16[256,256]{1,0:T(8,128)(2,1)S(1)}, bf16[256,256]{1,0:T(8,128)(2,1)S(1)}, u32[]{:S(2)}, u32[]{:S(2)}) collective-permute-start(bf16[256,256]{1,0:T(8,128)(2,1)S(1)} %get-tuple-element.61), channel_id=1, source_target_pairs={{0,8},{8,16},{16,24},{24,28},{28,20},{20,12},{12,4},{4,0},{1,9},{9... | collective-permute-start | bytes 393224 | tf_op jit(solution)/shard_map/ppermute | solution.py:401
  47.8 3.8 %shard_map.99 = (f32[512,256]{1,0:T(8,128)S(1)}, f32[512,256]{1,0:T(8,128)S(1)}, f32[4,1024,128]{2,1,0:T(8,128)S(1)}) custom-call(s32[2,8]{1,0:T(2,128)S(1)} %broadcast_add_fusion.tbl, bf16[4,1024,128]{2,1,0:T(8,128)(2,1)S(1)} %get-tuple-element.36.q_ref, bf16[4,1024,128]{2,1,0:T(8,128)(2,1)S(1)} %get-tuple-element.37.o_ref, ...), custom_call_target="tpu_custom_call" | custom-call | flops 1342177280 | bytes 1048576 | tf_op jit(solution)/shard_map/pallas_call | solution.py:51
  51.7 1.5 %collective-permute-start.9 = (bf16[512,256]{1,0:T(8,128)(2,1)S(1)}, bf16[512,256]{1,0:T(8,128)(2,1)S(1)}, u32[]{:S(2)}, u32[]{:S(2)}) collective-permute-start(bf16[512,256]{1,0:T(8,128)(2,1)S(1)} %pad_maximum_fusion), channel_id=1, source_target_pairs={{0,8},{8,16},{16,24},{24,28},{28,20},{20,12},{12,4},{4,0},{1,9},{9... | collective-permute-start | bytes 786440 | tf_op jit(solution)/shard_map/ppermute | solution.py:401
  53.9 3.8 %shard_map.100 = (f32[512,256]{1,0:T(8,128)S(1)}, f32[512,256]{1,0:T(8,128)S(1)}, f32[4,1024,128]{2,1,0:T(8,128)S(1)}) custom-call(s32[2,8]{1,0:T(2,128)S(1)} %broadcast_add_fusion.tbl, bf16[4,1024,128]{2,1,0:T(8,128)(2,1)S(1)} %get-tuple-element.36.q_ref, bf16[4,1024,128]{2,1,0:T(8,128)(2,1)S(1)} %get-tuple-element.37.o_ref, ...), custom_call_target="tpu_custom_call" | custom-call | flops 1342177280 | bytes 1048576 | tf_op jit(solution)/shard_map/pallas_call | solution.py:51
  57.7 2.0 %collective-permute-done.9 = bf16[512,256]{1,0:T(8,128)(2,1)S(1)} collective-permute-done((bf16[512,256]{1,0:T(8,128)(2,1)S(1)}, bf16[512,256]{1,0:T(8,128)(2,1)S(1)}, u32[]{:S(2)}, u32[]{:S(2)}) %collective-permute-start.9) | collective-permute-done | bytes 262176 | tf_op jit(solution)/shard_map/ppermute | solution.py:401
  59.7 1.8 %collective-permute-start.10 = (bf16[512,256]{1,0:T(8,128)(2,1)S(1)}, bf16[512,256]{1,0:T(8,128)(2,1)S(1)}, u32[]{:S(2)}, u32[]{:S(2)}) collective-permute-start(bf16[512,256]{1,0:T(8,128)(2,1)S(1)} %add_convert_fusion.3), channel_id=1, source_target_pairs={{0,8},{8,16},{16,24},{24,28},{28,20},{20,12},{12,4},{4,0},{1,9},{9... | collective-permute-start | bytes 786440 | tf_op jit(solution)/shard_map/ppermute | solution.py:401
  62.2 3.8 %shard_map.101 = (f32[512,256]{1,0:T(8,128)S(1)}, f32[512,256]{1,0:T(8,128)S(1)}, f32[4,1024,128]{2,1,0:T(8,128)S(1)}) custom-call(s32[2,8]{1,0:T(2,128)S(1)} %broadcast_add_fusion.tbl, bf16[4,1024,128]{2,1,0:T(8,128)(2,1)S(1)} %get-tuple-element.36.q_ref, bf16[4,1024,128]{2,1,0:T(8,128)(2,1)S(1)} %get-tuple-element.37.o_ref, ...), custom_call_target="tpu_custom_call" | custom-call | flops 1342177280 | bytes 1048576 | tf_op jit(solution)/shard_map/pallas_call | solution.py:51
  66.0 2.6 %collective-permute-done.10 = bf16[512,256]{1,0:T(8,128)(2,1)S(1)} collective-permute-done((bf16[512,256]{1,0:T(8,128)(2,1)S(1)}, bf16[512,256]{1,0:T(8,128)(2,1)S(1)}, u32[]{:S(2)}, u32[]{:S(2)}) %collective-permute-start.10) | collective-permute-done | bytes 262176 | tf_op jit(solution)/shard_map/ppermute | solution.py:401
  68.6 2.1 %collective-permute-start.11 = (bf16[512,256]{1,0:T(8,128)(2,1)S(1)}, bf16[512,256]{1,0:T(8,128)(2,1)S(1)}, u32[]{:S(2)}, u32[]{:S(2)}) collective-permute-start(bf16[512,256]{1,0:T(8,128)(2,1)S(1)} %add_convert_fusion.2), channel_id=1, source_target_pairs={{0,8},{8,16},{16,24},{24,28},{28,20},{20,12},{12,4},{4,0},{1,9},{9... | collective-permute-start | bytes 786440 | tf_op jit(solution)/shard_map/ppermute | solution.py:401
  71.3 4.3 %shard_map.102 = (bf16[256,2048]{1,0:T(8,128)(2,1)}, bf16[256,2048]{1,0:T(8,128)(2,1)}, f32[512,256]{1,0:T(8,128)S(1)}) custom-call(s32[2,8]{1,0:T(2,128)S(1)} %broadcast_add_fusion.tbl, bf16[4,1024,128]{2,1,0:T(8,128)(2,1)S(1)} %get-tuple-element.36.q_ref, bf16[4,1024,128]{2,1,0:T(8,128)(2,1)S(1)} %get-tuple-element.37.o_ref, ...), custom_call_target="tpu_custom_call" | custom-call | flops 805306368 | bytes 1048576 | tf_op jit(solution)/shard_map/pallas_call | solution.py:51
  75.7 1.6 %collective-permute-done.15.b_ref = bf16[512,256]{1,0:T(8,128)(2,1)S(1)} collective-permute-done((bf16[512,256]{1,0:T(8,128)(2,1)S(1)}, bf16[512,256]{1,0:T(8,128)(2,1)S(1)}, u32[]{:S(2)}, u32[]{:S(2)}) %collective-permute-start.15) | collective-permute-done | bytes 262176 | tf_op jit(solution)/shard_map/ppermute | solution.py:401
  (45 shorter events, 10.0 us)
Async XLA Ops:
  0.6 0.9 %copy-start.2 = (bf16[256,256]{1,0:T(8,128)(2,1)S(1)}, bf16[256,256]{1,0:T(8,128)(2,1)}, u32[]{:S(2)}) copy-start(bf16[256,256]{1,0:T(8,128)(2,1)} %k_ref.1) | copy-start | bytes 393220
  1.5 0.9 %copy-start.3 = (bf16[256,256]{1,0:T(8,128)(2,1)S(1)}, bf16[256,256]{1,0:T(8,128)(2,1)}, u32[]{:S(2)}) copy-start(bf16[256,256]{1,0:T(8,128)(2,1)} %v_ref.1) | copy-start | bytes 393220
  2.8 9.4 %collective-permute-start.4 = (bf16[512,256]{1,0:T(8,128)(2,1)S(1)}, bf16[512,256]{1,0:T(8,128)(2,1)S(1)}, u32[]{:S(2)}, u32[]{:S(2)}) collective-permute-start(bf16[512,256]{1,0:T(8,128)(2,1)S(1)} %shard_map.93.kv_ref), channel_id=1, source_target_pairs={{8,0},{16,8},{24,16},{28,24},{20,28},{12,20},{4,12},{0,4},{9,1},{1... | collective-permute-start | bytes 786440 | tf_op jit(solution)/shard_map/ppermute | solution.py:401
  5.8 8.0 %collective-permute-start = (bf16[512,256]{1,0:T(8,128)(2,1)S(1)}, bf16[512,256]{1,0:T(8,128)(2,1)S(1)}, u32[]{:S(2)}, u32[]{:S(2)}) collective-permute-start(bf16[512,256]{1,0:T(8,128)(2,1)S(1)} %shard_map.93.kv_ref), channel_id=1, source_target_pairs={{0,8},{8,16},{16,24},{24,28},{28,20},{20,12},{12,4},{4,0},{1,9},{9... | collective-permute-start | bytes 786440 | tf_op jit(solution)/shard_map/ppermute | solution.py:401
  12.2 7.5 %collective-permute-start.5 = (bf16[512,256]{1,0:T(8,128)(2,1)S(1)}, bf16[512,256]{1,0:T(8,128)(2,1)S(1)}, u32[]{:S(2)}, u32[]{:S(2)}) collective-permute-start(bf16[512,256]{1,0:T(8,128)(2,1)S(1)} %collective-permute-done.4.a_ref), channel_id=1, source_target_pairs={{8,0},{16,8},{24,16},{28,24},{20,28},{12,20},{4,12},{0,4},{9,1},{1... | collective-permute-start | bytes 786440 | tf_op jit(solution)/shard_map/ppermute | solution.py:401
  13.8 7.2 %collective-permute-start.1 = (bf16[512,256]{1,0:T(8,128)(2,1)S(1)}, bf16[512,256]{1,0:T(8,128)(2,1)S(1)}, u32[]{:S(2)}, u32[]{:S(2)}) collective-permute-start(bf16[512,256]{1,0:T(8,128)(2,1)S(1)} %collective-permute-done.b_ref), channel_id=1, source_target_pairs={{0,8},{8,16},{16,24},{24,28},{28,20},{20,12},{12,4},{4,0},{1,9},{9... | collective-permute-start | bytes 786440 | tf_op jit(solution)/shard_map/ppermute | solution.py:401
  19.7 9.0 %collective-permute-start.6 = (bf16[512,256]{1,0:T(8,128)(2,1)S(1)}, bf16[512,256]{1,0:T(8,128)(2,1)S(1)}, u32[]{:S(2)}, u32[]{:S(2)}) collective-permute-start(bf16[512,256]{1,0:T(8,128)(2,1)S(1)} %collective-permute-done.5.a_ref), channel_id=1, source_target_pairs={{8,0},{16,8},{24,16},{28,24},{20,28},{12,20},{4,12},{0,4},{9,1},{1... | collective-permute-start | bytes 786440 | tf_op jit(solution)/shard_map/ppermute | solution.py:401
  21.0 9.1 %collective-permute-start.2 = (bf16[512,256]{1,0:T(8,128)(2,1)S(1)}, bf16[512,256]{1,0:T(8,128)(2,1)S(1)}, u32[]{:S(2)}, u32[]{:S(2)}) collective-permute-start(bf16[512,256]{1,0:T(8,128)(2,1)S(1)} %collective-permute-done.1.b_ref), channel_id=1, source_target_pairs={{0,8},{8,16},{16,24},{24,28},{28,20},{20,12},{12,4},{4,0},{1,9},{9... | collective-permute-start | bytes 786440 | tf_op jit(solution)/shard_map/ppermute | solution.py:401
  21.8 1.2 %copy-start = (bf16[256,2048]{1,0:T(8,128)(2,1)S(1)}, bf16[256,2048]{1,0:T(8,128)(2,1)}, u32[]{:S(2)}) copy-start(bf16[256,2048]{1,0:T(8,128)(2,1)} %q_in.1) | copy-start | bytes 3145732
  23.0 1.2 %copy-start.1 = (bf16[256,2048]{1,0:T(8,128)(2,1)S(1)}, bf16[256,2048]{1,0:T(8,128)(2,1)}, u32[]{:S(2)}) copy-start(bf16[256,2048]{1,0:T(8,128)(2,1)} %o_in.1) | copy-start | bytes 3145732
  28.7 11.9 %collective-permute-start.7 = (bf16[256,256]{1,0:T(8,128)(2,1)S(1)}, bf16[256,256]{1,0:T(8,128)(2,1)S(1)}, u32[]{:S(2)}, u32[]{:S(2)}) collective-permute-start(bf16[256,256]{1,0:T(8,128)(2,1)S(1)} %slice.27), channel_id=1, source_target_pairs={{8,0},{16,8},{24,16},{28,24},{20,28},{12,20},{4,12},{0,4},{9,1},{1... | collective-permute-start | bytes 393224 | tf_op jit(solution)/shard_map/ppermute | solution.py:401
  30.2 10.4 %collective-permute-start.3 = (bf16[256,256]{1,0:T(8,128)(2,1)S(1)}, bf16[256,256]{1,0:T(8,128)(2,1)S(1)}, u32[]{:S(2)}, u32[]{:S(2)}) collective-permute-start(bf16[256,256]{1,0:T(8,128)(2,1)S(1)} %slice.26), channel_id=1, source_target_pairs={{0,8},{8,16},{16,24},{24,28},{28,20},{20,12},{12,4},{4,0},{1,9},{9... | collective-permute-start | bytes 393224 | tf_op jit(solution)/shard_map/ppermute | solution.py:401
  45.7 5.9 %collective-permute-start.8 = (bf16[256,256]{1,0:T(8,128)(2,1)S(1)}, bf16[256,256]{1,0:T(8,128)(2,1)S(1)}, u32[]{:S(2)}, u32[]{:S(2)}) collective-permute-start(bf16[256,256]{1,0:T(8,128)(2,1)S(1)} %get-tuple-element.61), channel_id=1, source_target_pairs={{0,8},{8,16},{16,24},{24,28},{28,20},{20,12},{12,4},{4,0},{1,9},{9... | collective-permute-start | bytes 393224 | tf_op jit(solution)/shard_map/ppermute | solution.py:401
  47.2 6.0 %collective-permute-start.12 = (bf16[256,256]{1,0:T(8,128)(2,1)S(1)}, bf16[256,256]{1,0:T(8,128)(2,1)S(1)}, u32[]{:S(2)}, u32[]{:S(2)}) collective-permute-start(bf16[256,256]{1,0:T(8,128)(2,1)S(1)} %get-tuple-element.65), channel_id=1, source_target_pairs={{8,0},{16,8},{24,16},{28,24},{20,28},{12,20},{4,12},{0,4},{9,1},{1... | collective-permute-start | bytes 393224 | tf_op jit(solution)/shard_map/ppermute | solution.py:401
  51.7 8.0 %collective-permute-start.9 = (bf16[512,256]{1,0:T(8,128)(2,1)S(1)}, bf16[512,256]{1,0:T(8,128)(2,1)S(1)}, u32[]{:S(2)}, u32[]{:S(2)}) collective-permute-start(bf16[512,256]{1,0:T(8,128)(2,1)S(1)} %pad_maximum_fusion), channel_id=1, source_target_pairs={{0,8},{8,16},{16,24},{24,28},{28,20},{20,12},{12,4},{4,0},{1,9},{9... | collective-permute-start | bytes 786440 | tf_op jit(solution)/shard_map/ppermute | solution.py:401
  53.3 8.6 %collective-permute-start.13 = (bf16[512,256]{1,0:T(8,128)(2,1)S(1)}, bf16[512,256]{1,0:T(8,128)(2,1)S(1)}, u32[]{:S(2)}, u32[]{:S(2)}) collective-permute-start(bf16[512,256]{1,0:T(8,128)(2,1)S(1)} %pad_maximum_fusion.1), channel_id=1, source_target_pairs={{8,0},{16,8},{24,16},{28,24},{20,28},{12,20},{4,12},{0,4},{9,1},{1... | collective-permute-start | bytes 786440 | tf_op jit(solution)/shard_map/ppermute | solution.py:401
  59.7 8.8 %collective-permute-start.10 = (bf16[512,256]{1,0:T(8,128)(2,1)S(1)}, bf16[512,256]{1,0:T(8,128)(2,1)S(1)}, u32[]{:S(2)}, u32[]{:S(2)}) collective-permute-start(bf16[512,256]{1,0:T(8,128)(2,1)S(1)} %add_convert_fusion.3), channel_id=1, source_target_pairs={{0,8},{8,16},{16,24},{24,28},{28,20},{20,12},{12,4},{4,0},{1,9},{9... | collective-permute-start | bytes 786440 | tf_op jit(solution)/shard_map/ppermute | solution.py:401
  61.9 8.8 %collective-permute-start.14 = (bf16[512,256]{1,0:T(8,128)(2,1)S(1)}, bf16[512,256]{1,0:T(8,128)(2,1)S(1)}, u32[]{:S(2)}, u32[]{:S(2)}) collective-permute-start(bf16[512,256]{1,0:T(8,128)(2,1)S(1)} %add_convert_fusion.1), channel_id=1, source_target_pairs={{8,0},{16,8},{24,16},{28,24},{20,28},{12,20},{4,12},{0,4},{9,1},{1... | collective-permute-start | bytes 786440 | tf_op jit(solution)/shard_map/ppermute | solution.py:401
  68.6 7.0 %collective-permute-start.11 = (bf16[512,256]{1,0:T(8,128)(2,1)S(1)}, bf16[512,256]{1,0:T(8,128)(2,1)S(1)}, u32[]{:S(2)}, u32[]{:S(2)}) collective-permute-start(bf16[512,256]{1,0:T(8,128)(2,1)S(1)} %add_convert_fusion.2), channel_id=1, source_target_pairs={{0,8},{8,16},{16,24},{24,28},{28,20},{20,12},{12,4},{4,0},{1,9},{9... | collective-permute-start | bytes 786440 | tf_op jit(solution)/shard_map/ppermute | solution.py:401
  70.8 6.4 %collective-permute-start.15 = (bf16[512,256]{1,0:T(8,128)(2,1)S(1)}, bf16[512,256]{1,0:T(8,128)(2,1)S(1)}, u32[]{:S(2)}, u32[]{:S(2)}) collective-permute-start(bf16[512,256]{1,0:T(8,128)(2,1)S(1)} %add_convert_fusion), channel_id=1, source_target_pairs={{8,0},{16,8},{24,16},{28,24},{20,28},{12,20},{4,12},{0,4},{9,1},{1... | collective-permute-start | bytes 786440 | tf_op jit(solution)/shard_map/ppermute | solution.py:401

commit v2 on v0

v2 whole, which is shorter than its diff:
```python
import functools
import math

import jax
import jax.numpy as jnp
from jax import lax
from jax.experimental import pallas as pl
from jax.experimental.pallas import tpu as pltpu
from jax.sharding import PartitionSpec as P


QH = 64
KVH = 8
DH = 128
BLOCK = 128
GROUP = QH // KVH
ROWS = GROUP * BLOCK
SUB = 8

SCALE = 1.0 / math.sqrt(DH)
EXP2_SCALE = SCALE * math.log2(math.e)
VMEM_BYTES = 24 * 1024 * 1024
FIRST_PART = 1024
NEAR_PART = 1024
TURN_PART = 1024
BACK_PART = 1024

NT = (((1,), (1,)), ((), ()))
VMEM = pl.BlockSpec(memory_space=pltpu.VMEM)
SMEM = pl.BlockSpec(memory_space=pltpu.SMEM)
HBM = pl.BlockSpec(memory_space=pltpu.HBM)


def dot(a, b):
    return jnp.dot(a, b, preferred_element_type=jnp.float32)


def dot_t(a, b):
    return lax.dot_general(a, b, NT, preferred_element_type=jnp.float32)


def bf16(shape):
    return jax.ShapeDtypeStruct(shape, jnp.bfloat16)


def f32(shape):
    return jax.ShapeDtypeStruct(shape, jnp.float32)


def call(kernel, in_specs, out_shape, flops, args, scratch=(), out_specs=None, size=1 << 20):
    return pl.pallas_call(
        kernel,
        in_specs=in_specs,
        out_specs=out_specs or [VMEM] * len(out_shape),
        out_shape=out_shape,
        scratch_shapes=list(scratch),
        compiler_params=pltpu.CompilerParams(vmem_limit_bytes=VMEM_BYTES),
        cost_estimate=pl.CostEstimate(
            flops=int(flops), bytes_accessed=size, transcendentals=0
        ),
    )(*args)


def at(index, size):
    if isinstance(index, int):
        return pl.ds(index * size, size)
    return pl.ds(pl.multiple_of(index * size, size), size)


def slot(w):
    return w if isinstance(w, int) else jnp.maximum(w, 0)


def block_of(ref, w, h):
    return ref[at(slot(w), BLOCK), at(h, DH)]


def key_of(ref, w, h, own):
    return jnp.where(w >= 0, block_of(ref, w, h), own)


def keep(w, x):
    return jnp.where(w >= 0, x, jnp.zeros_like(x))


def value_t(v, w):
    return keep(w, jnp.concatenate([v.T, jnp.ones((2 * SUB, BLOCK), v.dtype)], axis=0))


def queries_of(ref, b, h, part):
    members = range(part.start // BLOCK, part.stop // BLOCK)
    return jnp.concatenate(
        [ref[at(b, BLOCK), at(h * GROUP + g, DH)] for g in members], axis=0
    )


def split(x):
    return x.reshape(x.shape[0] // SUB, SUB, x.shape[1])


def join(x):
    return x.reshape(x.shape[0] * SUB, x.shape[2])


def all_equal(x):
    return jnp.broadcast_to(jnp.sum(x, axis=0, keepdims=True), x.shape)


def largest(x):
    top = jnp.max(x, axis=0)
    return jnp.broadcast_to(jnp.max(top, axis=0, keepdims=True), top.shape)


def parts(size):
    return [slice(t, t + size) for t in range(0, ROWS, size)]


def staggered(combos, size, phases):
    waiting = [phases(c, part) for c in range(combos) for part in parts(size)]
    active = []
    while waiting or active:
        if waiting:
            active.append(waiting.pop(0))
        active = [g for g in active if next(g, "end") != "end"]


def eye(size):
    row = lax.broadcasted_iota(jnp.int32, (size, size), 0)
    return jnp.where(row == lax.broadcasted_iota(jnp.int32, (size, size), 1), 1.0, 0.0).astype(
        jnp.bfloat16
    )


def table_kernel(slots_ref, counts_ref, tbl):
    blk_dev, n = tbl.shape
    me = lax.axis_index("ctx")

    def place(index):
        half = lax.shift_right_logical(index, 1)
        return jnp.where(lax.bitwise_and(index, 1) == 0, half, n - 1 - half)

    for b in range(blk_dev):
        for j in range(n):
            tbl[b, j] = -1
        row = me * blk_dev + b
        for s in range(slots_ref.shape[0]):
            block = slots_ref[s, row]
            owner = lax.div(block, blk_dev)
            offset = lax.rem(place(owner) - place(me) + n, n)

            @pl.when(s < counts_ref[row])
            def _():
                tbl[b, offset] = block - owner * blk_dev


def table(blocks, counts, blk_dev, n):
    return call(
        table_kernel, [SMEM] * 2, [jax.ShapeDtypeStruct((blk_dev, n), jnp.int32)], 1e10,
        (blocks.T, counts), out_specs=[SMEM], size=1 << 26,
    )[0]


def first_kernel(heads, q_ref, o_ref, k_ref, v_ref, ot_ref, acc_ref, m_ref):
    unit = eye(DH)

    def phases(c, part):
        b, h = c // heads, c % heads
        k = block_of(k_ref, b, h)
        x = dot_t(k, queries_of(q_ref, b, h, part))
        turned = dot_t(unit, queries_of(o_ref, b, h, part))
        yield
        v = value_t(block_of(v_ref, b, h), 0)
        x = split(x * EXP2_SCALE)
        m = largest(x)
        m_ref[c, :, part] = m
        p = join(jnp.exp2(x - m)).astype(jnp.bfloat16)
        ot_ref[c, :, part] = turned.astype(jnp.bfloat16)
        yield
        acc_ref[c, :, part] = dot(v, p)[: DH + SUB]

    staggered(m_ref.shape[0], FIRST_PART, phases)


def first(q, o, k, v, combos, heads):
    return call(
        functools.partial(first_kernel, heads),
        [VMEM] * 4,
        [bf16((combos, DH, ROWS)), f32((combos, DH + SUB, ROWS)), f32((combos, SUB, ROWS))],
        6 * combos * ROWS * BLOCK * DH,
        (q, o, k, v),
    )


def near_kernel(
    heads, ja, jb, tbl, q_ref, own_ref, ka_ref, va_ref, kb_ref, vb_ref, acc_in, m_in, acc_ref, m_ref
):
    def phases(c, part):
        b, h = c // heads, c % heads
        wa, wb = tbl[b, ja], tbl[b, jb]
        own = block_of(own_ref, b, h)
        k = jnp.concatenate([key_of(ka_ref, wa, h, own), key_of(kb_ref, wb, h, own)], axis=0)
        x = dot_t(k, queries_of(q_ref, b, h, part))
        yield
        v = jnp.concatenate(
            [value_t(block_of(va_ref, wa, h), wa), value_t(block_of(vb_ref, wb, h), wb)], axis=1
        )
        x = split(x * EXP2_SCALE)
        old = m_in[c, :, part]
        m = jnp.maximum(old, largest(x))
        p = join(jnp.exp2(x - m)).astype(jnp.bfloat16)
        m_ref[c, :, part] = m
        yield
        acc = join(split(acc_in[c, :, part]) * jnp.exp2(old - m))
        acc_ref[c, :, part] = acc + dot(v, p)[: DH + SUB]

    staggered(m_ref.shape[0], NEAR_PART, phases)


def near(tbl, q, k_own, ahead, behind, state, ja, jb, heads):
    combos = state[1].shape[0]
    return call(
        functools.partial(near_kernel, heads, ja, jb),
        [SMEM] + [VMEM] * 8,
        [f32(a.shape) for a in state],
        8 * combos * ROWS * BLOCK * DH,
        (tbl, q, k_own, *ahead, *behind, *state),
    )


def turn_kernel(
    heads, opposite, tbl, q_ref, o_ref, ot_ref, own_ref, k_ref, v_ref, acc_in, m_in,
    att_ref, lse_ref, delta_ref, ds_ref, pk_ref, pv_ref, pk_scr, pv_scr,
):
    pk_scr[...] = jnp.zeros_like(pk_scr)
    pv_scr[...] = jnp.zeros_like(pv_scr)

    def phases(c, part):
        b, h = c // heads, c % heads
        w = tbl[b, opposite]
        k = key_of(k_ref, w, h, block_of(own_ref, b, h))
        v = block_of(v_ref, w, h)
        q, o = queries_of(q_ref, b, h, part), queries_of(o_ref, b, h, part)
        x = dot_t(k, q)
        yield
        grad_p = split(dot_t(v, o))
        v_t = value_t(v, w)
        x = split(x * EXP2_SCALE)
        old = m_in[c, :, part]
        m = jnp.maximum(old, largest(x))
        p = jnp.exp2(x - m)
        acc = dot(v_t, join(p).astype(jnp.bfloat16))[: DH + SUB]
        yield
        acc = split(acc_in[c, :, part]) * jnp.exp2(old - m) + split(acc)
        total = acc[DH // SUB]
        inverse = 1.0 / total
        att = join(acc[: DH // SUB] * inverse).astype(jnp.bfloat16)
        att_ref[c, :, part] = att
        terms = att.astype(jnp.float32) * ot_ref[c, :, part].astype(jnp.float32)
        delta = all_equal(jnp.sum(split(terms), axis=0))
        p = p * inverse
        weights = join(p).astype(jnp.bfloat16)
        ds = join(p * (grad_p - delta)).astype(jnp.bfloat16)
        ds_ref[c, :, part] = ds
        lse_ref[c, :, part] = m + jnp.log2(total)
        delta_ref[c, :, part] = delta
        yield
        pk_scr[at(slot(w), BLOCK), h * DH : (h + 1) * DH] += keep(w, dot(ds, q))
        pv_scr[at(slot(w), BLOCK), h * DH : (h + 1) * DH] += keep(w, dot(weights, o))

    staggered(m_in.shape[0], TURN_PART, phases)
    pk_ref[...] = pk_scr[...].astype(jnp.bfloat16)
    pv_ref[...] = pv_scr[...].astype(jnp.bfloat16)


def turn(tbl, q, o, ot, k_own, k4, v4, state, opposite, heads):
    combos = ot.shape[0]
    return call(
        functools.partial(turn_kernel, heads, opposite),
        [SMEM] + [VMEM] * 8,
        [bf16(ot.shape)]
        + [f32((combos, SUB, ROWS))] * 2
        + [bf16((combos, BLOCK, ROWS))]
        + [bf16(k4.shape)] * 2,
        10 * combos * ROWS * BLOCK * DH,
        (tbl, q, o, ot, k_own, k4, v4, *state),
        [pltpu.VMEM(k4.shape, jnp.float32)] * 2,
    )


def weights_and_grads(c, part, x, grad_p, lse_ref, delta_ref):
    p = jnp.exp2(split(x * EXP2_SCALE) - lse_ref[c, :, part])
    ds = p * (split(grad_p) - delta_ref[c, :, part])
    return join(p).astype(jnp.bfloat16), join(ds).astype(jnp.bfloat16)


def back_kernel(
    heads, ja, jb, has_sum, tbl, q_ref, o_ref, own_ref, lse_ref, delta_ref, ka_ref, va_ref,
    kb_ref, vb_ref, *refs,
):
    if has_sum:
        gq_in, *refs = refs
    pka_ref, pva_ref, pkb_ref, pvb_ref, gq_ref = refs
    for ref in (pka_ref, pva_ref, pkb_ref, pvb_ref):
        ref[...] = jnp.zeros_like(ref)

    def phases(c, part):
        b, h = c // heads, c % heads
        wa, wb = tbl[b, ja], tbl[b, jb]
        own = block_of(own_ref, b, h)
        ka, kb = key_of(ka_ref, wa, h, own), key_of(kb_ref, wb, h, own)
        v = jnp.concatenate([block_of(va_ref, wa, h), block_of(vb_ref, wb, h)], axis=0)
        q, o = queries_of(q_ref, b, h, part), queries_of(o_ref, b, h, part)
        x = dot_t(jnp.concatenate([ka, kb], axis=0), q)
        grad_p = dot_t(v, o)
        yield
        weights, ds = weights_and_grads(c, part, x, grad_p, lse_ref, delta_ref)
        yield
        dk, dv = dot(ds, q), dot(weights, o)
        lanes = slice(h * DH, (h + 1) * DH)
        for i, (rk, rv, w) in enumerate(((pka_ref, pva_ref, wa), (pkb_ref, pvb_ref, wb))):
            src = slice(i * BLOCK, (i + 1) * BLOCK)
            rk[at(slot(w), BLOCK), lanes] += keep(w, dk[src])
            rv[at(slot(w), BLOCK), lanes] += keep(w, dv[src])
        grad = dot(jnp.concatenate([keep(wa, ka).T, keep(wb, kb).T], axis=1), ds)
        gq_ref[c, :, part] = gq_in[c, :, part] + grad if has_sum else grad

    staggered(gq_ref.shape[0], BACK_PART, phases)


def back(tbl, q, o, k_own, stats, ahead, behind, gq, ja, jb, heads):
    combos = stats[0].shape[0]
    extra = () if gq is None else (gq,)
    return call(
        functools.partial(back_kernel, heads, ja, jb, gq is not None),
        [SMEM] + [VMEM] * (9 + len(extra)),
        [f32(k_own.shape)] * 4 + [f32((combos, DH, ROWS))],
        20 * combos * ROWS * BLOCK * DH,
        (tbl, q, o, k_own, *stats, *ahead, *behind, *extra),
    )


def own_kernel(
    heads, opposite, tbl, q_ref, o_ref, k_ref, v_ref, lse_ref, delta_ref, k4_ref, ds4_ref,
    att_ref, gq_in, att_out, gq_out, pk_ref, pv_ref, att_scr, gq_scr, sems,
):
    combos = gq_in.shape[0]
    unit = eye(2 * BLOCK)

    def send(ref, out, c, kind):
        b, h = c // heads, c % heads
        place = (at(b, BLOCK), at(h, GROUP * DH))
        return pltpu.make_async_copy(ref.at[place], out.at[place], sems.at[kind, c])

    def put(ref, b, h, x):
        for i in range(GROUP // 2):
            y = dot_t(unit, x[:, i * 2 * BLOCK : (i + 1) * 2 * BLOCK]).astype(jnp.bfloat16)
            for j in range(2):
                place = (at(b, BLOCK), at(h * GROUP + 2 * i + j, DH))
                ref[place] = y[j * BLOCK : (j + 1) * BLOCK]

    def phases(c, part):
        b, h = c // heads, c % heads
        q, o = queries_of(q_ref, b, h, part), queries_of(o_ref, b, h, part)
        k = block_of(k_ref, b, h)
        x, grad_p = dot_t(k, q), dot_t(block_of(v_ref, b, h), o)
        yield
        weights, ds = weights_and_grads(c, part, x, grad_p, lse_ref, delta_ref)
        put(att_scr, b, h, att_ref[c])
        send(att_scr, att_out, c, 0).start()
        yield
        place = (at(b, BLOCK), at(h, DH))
        pk_ref[place] = dot(ds, q)
        pv_ref[place] = dot(weights, o)
        w4 = tbl[b, opposite]
        used = jnp.concatenate([k.T, keep(w4, block_of(k4_ref, w4, h)).T], axis=1)
        grad = (gq_in[c] + dot(used, jnp.concatenate([ds, ds4_ref[c]], axis=0))) * SCALE
        yield
        put(gq_scr, b, h, grad.astype(jnp.bfloat16))
        send(gq_scr, gq_out, c, 1).start()

    staggered(combos, ROWS, phases)
    for c in range(combos):
        send(att_scr, att_out, c, 0).wait()
        send(gq_scr, gq_out, c, 1).wait()


def own(tbl, q, o, k, v, stats, k4, ds4, att, gq, opposite, heads):
    combos = gq.shape[0]
    return call(
        functools.partial(own_kernel, heads, opposite),
        [SMEM] + [VMEM] * 10,
        [bf16(q.shape), bf16(q.shape), f32(k.shape), f32(k.shape)],
        12 * combos * ROWS * BLOCK * DH,
        (tbl, q, o, k, v, *stats, k4, ds4, att, gq),
        [pltpu.VMEM(q.shape, jnp.bfloat16)] * 2
        + [pltpu.SemaphoreType.DMA((2, combos))],
        [HBM, HBM, VMEM, VMEM],
    )


def finish_kernel(pk_ref, ka_ref, kb_ref, pv_ref, va_ref, vb_ref, gk_ref, gv_ref):
    def total(own, a, b):
        return own[...] + (a[...].astype(jnp.float32) + b[...].astype(jnp.float32))

    gk_ref[...] = (total(pk_ref, ka_ref, kb_ref) * SCALE).astype(jnp.bfloat16)
    gv_ref[...] = total(pv_ref, va_ref, vb_ref).astype(jnp.bfloat16)


def finish(*args):
    return call(finish_kernel, [VMEM] * 6, [bf16(args[0].shape)] * 2, 1e7, args)


def local(queries, keys, values, grad_out, key_blocks, key_count):
    n = lax.axis_size("ctx")
    row_count, width = keys.shape
    blk_dev = row_count // BLOCK
    heads = width // DH
    combos = blk_dev * heads
    opposite = n // 2
    steps = opposite - 1

    order = list(range(0, n, 2)) + list(range(n - 1, 0, -2))
    up = [(order[i], order[(i + 1) % n]) for i in range(n)]
    ways = {"up": up, "down": [(b, a) for a, b in up]}

    def hop(x, way):
        return lax.ppermute(x, "ctx", ways[way])

    behind, ahead = [(keys, values)], [(keys, values)]
    tbl = table(key_blocks, key_count, blk_dev, n)
    ot, *state = first(queries, grad_out, keys, values, combos, heads)
    for s in range(1, steps + 1):
        k_up = hop(behind[-1][0], "up")
        k_down = hop(ahead[-1][0], "down")
        v_up = hop(behind[-1][1], "up")
        v_down = hop(ahead[-1][1], "down")
        behind.append((k_up, v_up))
        ahead.append((k_down, v_down))
        state = near(
            tbl, queries, keys, ahead[s], behind[s], state, s, n - s, heads
        )
    k4 = hop(behind[-1][0], "up")
    v4 = hop(ahead[-1][1], "down")

    att, lse, delta, ds4, pk, pv = turn(
        tbl, queries, grad_out, ot, keys, k4, v4, state, opposite, heads
    )
    stats = (lse, delta)

    def plus(part, x):
        return part if x is None else part + x.astype(jnp.float32)

    k_up, k_down = hop(pk, "up"), None
    v_up, v_down = None, hop(pv, "down")
    gq = None
    for s in range(steps, 0, -1):
        pka, pva, pkb, pvb, gq = back(
            tbl, queries, grad_out, keys, stats, ahead[s], behind[s], gq, s, n - s, heads
        )
        k_up = hop(plus(pka, k_up).astype(jnp.bfloat16), "up")
        k_down = hop(plus(pkb, k_down).astype(jnp.bfloat16), "down")
        v_up = hop(plus(pva, v_up).astype(jnp.bfloat16), "up")
        v_down = hop(plus(pvb, v_down).astype(jnp.bfloat16), "down")
    attended, grad_q, pk, pv = own(
        tbl, queries, grad_out, keys, values, stats, k4, ds4, att, gq, opposite, heads
    )
    grad_k, grad_v = finish(pk, k_up, k_down, pv, v_up, v_down)
    return attended, grad_q, grad_k, grad_v


def solution(mesh):
    spec = P("ctx", "head")
    return jax.shard_map(
        local,
        mesh=mesh,
        in_specs=(spec, spec, spec, spec, P(), P()),
        out_specs=(spec,) * 4,
        check_vma=False,
    )
```

time: 280 us -> 69.3 us (0.25)
  waiting for transfers between devices: 133 us -> 7.17 us
  local copies, waits for them, and re-layouts: 64.8 us -> 1.36 us
  matrix products: 55.9 us -> 0 us
  Pallas kernels: 0 us -> 28.4 us
  starting transfers between devices: 12.2 us -> 31 us
  other arithmetic: 11.7 us -> 0.37 us
    all_to_all x2 -> x0, waiting for transfers between devices: 133 us -> none  [the longest x1 88.1 us: local(): lax.all_to_all(outgoing_sums, 'ctx', split_axis=0, concat_axis=0, tiled=T...]
    dot_general x14 -> x0, matrix products: 41.8 us -> none  [the longest x2 13.3 us: attend(): jnp.einsum('qhgd,khd->hgqk', o_blk, near_v, preferred_element_type=jnp.fl...]
    ppermute x0 -> x28, starting transfers between devices: none -> 31 us  [hop(): return lax.ppermute(x, 'ctx', ways[way])]
    pallas_call x0 -> x11, Pallas kernels: none -> 28.4 us  [call(): pl.pallas_call(kernel, in_specs=in_specs, out_specs=out_specs or [VMEM] *...]
    reshape x19 -> x0, local copies, waits for them, and re-layouts: 24.1 us -> none  [the longest x1 4.32 us: local(): part_k = part_k.reshape(blk_dev, KSLOTS + 1, tile_size)]
    dynamic_update_slice x12 -> x0, local copies, waits for them, and re-layouts: 14.2 us -> none  [local(): lax.map(per_block, (q_tiles, o_tiles, near_k, near_v, columns))]
    sub x2 -> x0, matrix products: 14.1 us -> none  [attend(): expo_terms = jnp.where(column, jnp.exp(scores - row_max), 0.0)]
    all_to_all x2 -> x0, starting transfers between devices: 12.2 us -> none  [the longest x1 7.41 us: local(): lax.all_to_all(outgoing, 'ctx', split_axis=0, concat_axis=0, tiled=True)]
  transfers between devices with their start and end apart: 2 -> 28, of which waited for: 2 -> 6; matrix products, arithmetic and copies ran while one was open for 3% -> 1% of each run, Pallas kernels for 0% -> 35%
where the time goes in v2:
time: 69.3 us; the launch traced here: 69.1 us
  starting transfers between devices  31 us (45%)
  Pallas kernels  28.4 us (41%)
  waiting for transfers between devices  7.17 us (10%)
  local copies, waits for them, and re-layouts  1.36 us (2%)
  between operations  0.87 us (1%)
    ppermute x28, starting transfers between devices, hop(): return lax.ppermute(x, 'ctx', ways[way])  31 us
    pallas_call x11, Pallas kernels, call(): pl.pallas_call(kernel, in_specs=in_specs, out_specs=out_specs or [VMEM] *...  28.4 us
    ppermute x28, waiting for transfers between devices, hop(): return lax.ppermute(x, 'ctx', ways[way])  7.17 us
  transfers between devices with their start and end apart: 28, of which 6 were waited for; matrix products, arithmetic and copies ran while one was open for 1% of the time, Pallas kernels for 35%

profile of v2, /device:TPU:0, one launch (start us, length us, event | category | flops | bytes accessed | tf_op | source)
XLA Modules:
  0.0 69.1 jit_solution(120903239218535145)
XLA Ops:
  0.6 3.0 %collective-permute-start.4 = (bf16[256,256]{1,0:T(8,128)(2,1)}, bf16[256,256]{1,0:T(8,128)(2,1)S(1)}, u32[]{:S(2)}, u32[]{:S(2)}) collective-permute-start(bf16[256,256]{1,0:T(8,128)(2,1)} %v_ref.3), channel_id=1, source_target_pairs={{8,0},{16,8},{24,16},{28,24},{20,28},{12,20},{4,12},{0,4},{9,1},{1... | collective-permute-start | bytes 393224 | tf_op jit(solution)/shard_map/ppermute | solution.py:427
  3.8 2.0 %collective-permute-start.11 = (bf16[256,256]{1,0:T(8,128)(2,1)}, bf16[256,256]{1,0:T(8,128)(2,1)S(1)}, u32[]{:S(2)}, u32[]{:S(2)}) collective-permute-start(bf16[256,256]{1,0:T(8,128)(2,1)} %v_ref.3), channel_id=1, source_target_pairs={{0,8},{8,16},{16,24},{24,28},{28,20},{20,12},{12,4},{4,0},{1,9},{9... | collective-permute-start | bytes 393224 | tf_op jit(solution)/shard_map/ppermute | solution.py:427
  5.8 2.0 %collective-permute-done.4.va_ref = bf16[256,256]{1,0:T(8,128)(2,1)S(1)} collective-permute-done((bf16[256,256]{1,0:T(8,128)(2,1)}, bf16[256,256]{1,0:T(8,128)(2,1)S(1)}, u32[]{:S(2)}, u32[]{:S(2)}) %collective-permute-start.4) | collective-permute-done | bytes 131104 | tf_op jit(solution)/shard_map/ppermute | solution.py:427
  7.9 2.4 %collective-permute-start.5 = (bf16[256,256]{1,0:T(8,128)(2,1)S(1)}, bf16[256,256]{1,0:T(8,128)(2,1)S(1)}, u32[]{:S(2)}, u32[]{:S(2)}) collective-permute-start(bf16[256,256]{1,0:T(8,128)(2,1)S(1)} %collective-permute-done.4.va_ref), channel_id=1, source_target_pairs={{8,0},{16,8},{24,16},{28,24},{20,28},{12,20},{4,12},{0,4},{9,1},{1... | collective-permute-start | bytes 393224 | tf_op jit(solution)/shard_map/ppermute | solution.py:427
  10.4 2.5 %collective-permute-done.11.vb_ref = bf16[256,256]{1,0:T(8,128)(2,1)S(1)} collective-permute-done((bf16[256,256]{1,0:T(8,128)(2,1)}, bf16[256,256]{1,0:T(8,128)(2,1)S(1)}, u32[]{:S(2)}, u32[]{:S(2)}) %collective-permute-start.11) | collective-permute-done | bytes 131104 | tf_op jit(solution)/shard_map/ppermute | solution.py:427
  13.1 1.8 %collective-permute-start.9 = (bf16[256,256]{1,0:T(8,128)(2,1)S(1)}, bf16[256,256]{1,0:T(8,128)(2,1)S(1)}, u32[]{:S(2)}, u32[]{:S(2)}) collective-permute-start(bf16[256,256]{1,0:T(8,128)(2,1)S(1)} %collective-permute-done.8.ka_ref), channel_id=1, source_target_pairs={{8,0},{16,8},{24,16},{28,24},{20,28},{12,20},{4,12},{0,4},{9,1},{1... | collective-permute-start | bytes 393224 | tf_op jit(solution)/shard_map/ppermute | solution.py:427
  14.9 1.6 %collective-permute-start.6 = (bf16[256,256]{1,0:T(8,128)(2,1)S(1)}, bf16[256,256]{1,0:T(8,128)(2,1)S(1)}, u32[]{:S(2)}, u32[]{:S(2)}) collective-permute-start(bf16[256,256]{1,0:T(8,128)(2,1)S(1)} %collective-permute-done.5.va_ref), channel_id=1, source_target_pairs={{8,0},{16,8},{24,16},{28,24},{20,28},{12,20},{4,12},{0,4},{9,1},{1... | collective-permute-start | bytes 393224 | tf_op jit(solution)/shard_map/ppermute | solution.py:427
  18.3 1.3 %shard_map.93.tbl = s32[2,8]{1,0:T(2,128)S(1)} custom-call(s32[6,16]{1,0:T(8,128)S(1)} %bitcast.1, s32[16]{0:T(128)S(1)} %copy-done.5), custom_call_target="tpu_custom_call" | custom-call | flops 10000000000 | bytes 67108864 | tf_op jit(solution)/shard_map/pallas_call | solution.py:51
  22.8 1.6 %collective-permute-start.7 = (bf16[256,256]{1,0:T(8,128)(2,1)S(1)}, bf16[256,256]{1,0:T(8,128)(2,1)S(1)}, u32[]{:S(2)}, u32[]{:S(2)}) collective-permute-start(bf16[256,256]{1,0:T(8,128)(2,1)S(1)} %collective-permute-done.6.va_ref), channel_id=1, source_target_pairs={{8,0},{16,8},{24,16},{28,24},{20,28},{12,20},{4,12},{0,4},{9,1},{1... | collective-permute-start | bytes 393224 | tf_op jit(solution)/shard_map/ppermute | solution.py:427
  24.9 2.4 %shard_map.95 = (f32[4,136,1024]{2,1,0:T(8,128)S(1)}, f32[4,8,1024]{2,1,0:T(8,128)S(1)}) custom-call(s32[2,8]{1,0:T(2,128)S(1)} %shard_map.93.tbl, bf16[256,2048]{1,0:T(8,128)(2,1)S(1)} %copy-done, bf16[256,256]{1,0:T(8,128)(2,1)S(1)} %copy-done.2, bf16[256,256]{1,0:T(8,128)(2,1)S(1)} %collective-permute-done.8.ka_ref, ...), custom_call_target="tpu_custom_call" | custom-call | flops 536870912 | bytes 1048576 | tf_op jit(solution)/shard_map/pallas_call | solution.py:51
  27.4 2.4 %shard_map.96 = (f32[4,136,1024]{2,1,0:T(8,128)S(1)}, f32[4,8,1024]{2,1,0:T(8,128)S(1)}) custom-call(s32[2,8]{1,0:T(2,128)S(1)} %shard_map.93.tbl, bf16[256,2048]{1,0:T(8,128)(2,1)S(1)} %copy-done, bf16[256,256]{1,0:T(8,128)(2,1)S(1)} %copy-done.2, bf16[256,256]{1,0:T(8,128)(2,1)S(1)} %collective-permute-done.9.ka_ref, ...), custom_call_target="tpu_custom_call" | custom-call | flops 536870912 | bytes 1048576 | tf_op jit(solution)/shard_map/pallas_call | solution.py:51
  29.8 2.4 %shard_map.97 = (f32[4,136,1024]{2,1,0:T(8,128)S(1)}, f32[4,8,1024]{2,1,0:T(8,128)S(1)}) custom-call(s32[2,8]{1,0:T(2,128)S(1)} %shard_map.93.tbl, bf16[256,2048]{1,0:T(8,128)(2,1)S(1)} %copy-done, bf16[256,256]{1,0:T(8,128)(2,1)S(1)} %copy-done.2, bf16[256,256]{1,0:T(8,128)(2,1)S(1)} %collective-permute-done.10.ka_ref, ...), custom_call_target="tpu_custom_call" | custom-call | flops 536870912 | bytes 1048576 | tf_op jit(solution)/shard_map/pallas_call | solution.py:51
  32.3 3.6 %shard_map.98 = (bf16[4,128,1024]{2,1,0:T(8,128)(2,1)S(1)}, f32[4,8,1024]{2,1,0:T(8,128)S(1)}, f32[4,8,1024]{2,1,0:T(8,128)S(1)}, bf16[4,128,1024]{2,1,0:T(8,128...) custom-call(s32[2,8]{1,0:T(2,128)S(1)} %shard_map.93.tbl, bf16[256,2048]{1,0:T(8,128)(2,1)S(1)} %copy-done, ...), custom_call_target="tpu_custom_call" | custom-call | flops 671088640 | bytes 1048576 | tf_op jit(solution)/shard_map/pallas_call | solution.py:51
  35.9 1.2 %collective-permute-start.14 = (bf16[256,256]{1,0:T(8,128)(2,1)S(1)}, bf16[256,256]{1,0:T(8,128)(2,1)S(1)}, u32[]{:S(2)}, u32[]{:S(2)}) collective-permute-start(bf16[256,256]{1,0:T(8,128)(2,1)S(1)} %get-tuple-element.62), channel_id=1, source_target_pairs={{0,8},{8,16},{16,24},{24,28},{28,20},{20,12},{12,4},{4,0},{1,9},{9... | collective-permute-start | bytes 393224 | tf_op jit(solution)/shard_map/ppermute | solution.py:427
  38.0 3.4 %shard_map.99 = (f32[256,256]{1,0:T(8,128)S(1)}, f32[256,256]{1,0:T(8,128)S(1)}, f32[256,256]{1,0:T(8,128)S(1)}, f32[256,256]{1,0:T(8,128)S(1)}, f32[4,128,1024]{2,1,0:T(8,128)S(1)}) custom-call(s32[2,8]{1,0:T(2,128)S(1)} %shard_map.93.tbl, bf16[256,2048]{1,0:T(8,128)(2,1)S(1)} %copy-done, bf16[256,2048]{1,0:T(8,128)(2,1)S(1)} %copy-done.1, ...), custom_call_target="tpu_custom_call" | custom-call | flops 1342177280 | bytes 1048576 | tf_op jit(solution)/shard_map/pallas_call | solution.py:51
  41.4 1.2 %collective-permute-start.21 = (bf16[256,256]{1,0:T(8,128)(2,1)S(1)}, bf16[256,256]{1,0:T(8,128)(2,1)S(1)}, u32[]{:S(2)}, u32[]{:S(2)}) collective-permute-start(bf16[256,256]{1,0:T(8,128)(2,1)S(1)} %convert_element_type.77), channel_id=1, source_target_pairs={{0,8},{8,16},{16,24},{24,28},{28,20},{20,12},{12,4},{4,0},{1,9},{9... | collective-permute-start | bytes 393224 | tf_op jit(solution)/shard_map/ppermute | solution.py:427
  43.5 3.4 %shard_map.100 = (f32[256,256]{1,0:T(8,128)S(1)}, f32[256,256]{1,0:T(8,128)S(1)}, f32[256,256]{1,0:T(8,128)S(1)}, f32[256,256]{1,0:T(8,128)S(1)}, f32[4,128,1024]{2,1,0:T(8,128)S(1)}) custom-call(s32[2,8]{1,0:T(2,128)S(1)} %shard_map.93.tbl, bf16[256,2048]{1,0:T(8,128)(2,1)S(1)} %copy-done, bf16[256,2048]{1,0:T(8,128)(2,1)S(1)} %copy-done.1, ...), custom_call_target="tpu_custom_call" | custom-call | flops 1342177280 | bytes 1048576 | tf_op jit(solution)/shard_map/pallas_call | solution.py:51
  46.9 3.4 %shard_map.101 = (f32[256,256]{1,0:T(8,128)S(1)}, f32[256,256]{1,0:T(8,128)S(1)}, f32[256,256]{1,0:T(8,128)S(1)}, f32[256,256]{1,0:T(8,128)S(1)}, f32[4,128,1024]{2,1,0:T(8,128)S(1)}) custom-call(s32[2,8]{1,0:T(2,128)S(1)} %shard_map.93.tbl, bf16[256,2048]{1,0:T(8,128)(2,1)S(1)} %copy-done, bf16[256,2048]{1,0:T(8,128)(2,1)S(1)} %copy-done.1, ...), custom_call_target="tpu_custom_call" | custom-call | flops 1342177280 | bytes 1048576 | tf_op jit(solution)/shard_map/pallas_call | solution.py:51
  52.5 1.6 %collective-permute-start.19 = (bf16[256,256]{1,0:T(8,128)(2,1)S(1)}, bf16[256,256]{1,0:T(8,128)(2,1)S(1)}, u32[]{:S(2)}, u32[]{:S(2)}) collective-permute-start(bf16[256,256]{1,0:T(8,128)(2,1)S(1)} %add_convert_fusion.6), channel_id=1, source_target_pairs={{8,0},{16,8},{24,16},{28,24},{20,28},{12,20},{4,12},{0,4},{9,1},{1... | collective-permute-start | bytes 393224 | tf_op jit(solution)/shard_map/ppermute | solution.py:427
  54.7 1.7 %collective-permute-done.15 = bf16[256,256]{1,0:T(8,128)(2,1)S(1)} collective-permute-done((bf16[256,256]{1,0:T(8,128)(2,1)S(1)}, bf16[256,256]{1,0:T(8,128)(2,1)S(1)}, u32[]{:S(2)}, u32[]{:S(2)}) %collective-permute-start.15) | collective-permute-done | bytes 131104 | tf_op jit(solution)/shard_map/ppermute | solution.py:427
  57.3 1.3 %collective-permute-start.26 = (bf16[256,256]{1,0:T(8,128)(2,1)S(1)}, bf16[256,256]{1,0:T(8,128)(2,1)S(1)}, u32[]{:S(2)}, u32[]{:S(2)}) collective-permute-start(bf16[256,256]{1,0:T(8,128)(2,1)S(1)} %add_convert_fusion.1), channel_id=1, source_target_pairs={{8,0},{16,8},{24,16},{28,24},{20,28},{12,20},{4,12},{0,4},{9,1},{1... | collective-permute-start | bytes 393224 | tf_op jit(solution)/shard_map/ppermute | solution.py:427
  59.1 1.4 %collective-permute-start.20 = (bf16[256,256]{1,0:T(8,128)(2,1)S(1)}, bf16[256,256]{1,0:T(8,128)(2,1)S(1)}, u32[]{:S(2)}, u32[]{:S(2)}) collective-permute-start(bf16[256,256]{1,0:T(8,128)(2,1)S(1)} %add_convert_fusion.5), channel_id=1, source_target_pairs={{8,0},{16,8},{24,16},{28,24},{20,28},{12,20},{4,12},{0,4},{9,1},{1... | collective-permute-start | bytes 393224 | tf_op jit(solution)/shard_map/ppermute | solution.py:427
  61.6 1.5 %collective-permute-start.17 = (bf16[256,256]{1,0:T(8,128)(2,1)S(1)}, bf16[256,256]{1,0:T(8,128)(2,1)S(1)}, u32[]{:S(2)}, u32[]{:S(2)}) collective-permute-start(bf16[256,256]{1,0:T(8,128)(2,1)S(1)} %add_convert_fusion.7), channel_id=1, source_target_pairs={{0,8},{8,16},{16,24},{24,28},{28,20},{20,12},{12,4},{4,0},{1,9},{9... | collective-permute-start | bytes 393224 | tf_op jit(solution)/shard_map/ppermute | solution.py:427
  64.0 4.1 %shard_map.102 = (bf16[256,2048]{1,0:T(8,128)(2,1)}, bf16[256,2048]{1,0:T(8,128)(2,1)}, f32[256,256]{1,0:T(8,128)S(1)}, f32[256,256]{1,0:T(8,128)S(1)}) custom-call(s32[2,8]{1,0:T(2,128)S(1)} %shard_map.93.tbl, bf16[256,2048]{1,0:T(8,128)(2,1)S(1)} %copy-done, bf16[256,2048]{1,0:T(8,128)(2,1)S(1)} %copy-done.1, bf16[256,256]{1,0:T(8,128)(2,1)S(1)} %copy-done.2, ...), custom_call_target="tpu_custom_call" | custom-call | flops 805306368 | bytes 1048576 | tf_op jit(solution)/shard_map/pallas_call | solution.py:51
  (67 shorter events, 14.8 us)
Async XLA Ops:
  0.6 7.2 %collective-permute-start.4 = (bf16[256,256]{1,0:T(8,128)(2,1)}, bf16[256,256]{1,0:T(8,128)(2,1)S(1)}, u32[]{:S(2)}, u32[]{:S(2)}) collective-permute-start(bf16[256,256]{1,0:T(8,128)(2,1)} %v_ref.3), channel_id=1, source_target_pairs={{8,0},{16,8},{24,16},{28,24},{20,28},{12,20},{4,12},{0,4},{9,1},{1... | collective-permute-start | bytes 393224 | tf_op jit(solution)/shard_map/ppermute | solution.py:427
  3.7 6.6 %collective-permute-start = (bf16[256,256]{1,0:T(8,128)(2,1)}, bf16[256,256]{1,0:T(8,128)(2,1)S(1)}, u32[]{:S(2)}, u32[]{:S(2)}) collective-permute-start(bf16[256,256]{1,0:T(8,128)(2,1)} %k_ref.3), channel_id=1, source_target_pairs={{0,8},{8,16},{16,24},{24,28},{28,20},{20,12},{12,4},{4,0},{1,9},{9... | collective-permute-start | bytes 393224 | tf_op jit(solution)/shard_map/ppermute | solution.py:427
  3.8 9.1 %collective-permute-start.11 = (bf16[256,256]{1,0:T(8,128)(2,1)}, bf16[256,256]{1,0:T(8,128)(2,1)S(1)}, u32[]{:S(2)}, u32[]{:S(2)}) collective-permute-start(bf16[256,256]{1,0:T(8,128)(2,1)} %v_ref.3), channel_id=1, source_target_pairs={{0,8},{8,16},{16,24},{24,28},{28,20},{20,12},{12,4},{4,0},{1,9},{9... | collective-permute-start | bytes 393224 | tf_op jit(solution)/shard_map/ppermute | solution.py:427
  5.8 7.3 %collective-permute-start.8 = (bf16[256,256]{1,0:T(8,128)(2,1)}, bf16[256,256]{1,0:T(8,128)(2,1)S(1)}, u32[]{:S(2)}, u32[]{:S(2)}) collective-permute-start(bf16[256,256]{1,0:T(8,128)(2,1)} %k_ref.3), channel_id=1, source_target_pairs={{8,0},{16,8},{24,16},{28,24},{20,28},{12,20},{4,12},{0,4},{9,1},{1... | collective-permute-start | bytes 393224 | tf_op jit(solution)/shard_map/ppermute | solution.py:427
  7.9 7.0 %collective-permute-start.5 = (bf16[256,256]{1,0:T(8,128)(2,1)S(1)}, bf16[256,256]{1,0:T(8,128)(2,1)S(1)}, u32[]{:S(2)}, u32[]{:S(2)}) collective-permute-start(bf16[256,256]{1,0:T(8,128)(2,1)S(1)} %collective-permute-done.4.va_ref), channel_id=1, source_target_pairs={{8,0},{16,8},{24,16},{28,24},{20,28},{12,20},{4,12},{0,4},{9,1},{1... | collective-permute-start | bytes 393224 | tf_op jit(solution)/shard_map/ppermute | solution.py:427
  10.2 6.2 %collective-permute-start.1 = (bf16[256,256]{1,0:T(8,128)(2,1)S(1)}, bf16[256,256]{1,0:T(8,128)(2,1)S(1)}, u32[]{:S(2)}, u32[]{:S(2)}) collective-permute-start(bf16[256,256]{1,0:T(8,128)(2,1)S(1)} %collective-permute-done.kb_ref), channel_id=1, source_target_pairs={{0,8},{8,16},{16,24},{24,28},{28,20},{20,12},{12,4},{4,0},{1,9},{9... | collective-permute-start | bytes 393224 | tf_op jit(solution)/shard_map/ppermute | solution.py:427
  12.9 6.7 %collective-permute-start.12 = (bf16[256,256]{1,0:T(8,128)(2,1)S(1)}, bf16[256,256]{1,0:T(8,128)(2,1)S(1)}, u32[]{:S(2)}, u32[]{:S(2)}) collective-permute-start(bf16[256,256]{1,0:T(8,128)(2,1)S(1)} %collective-permute-done.11.vb_ref), channel_id=1, source_target_pairs={{0,8},{8,16},{16,24},{24,28},{28,20},{20,12},{12,4},{4,0},{1,9},{9... | collective-permute-start | bytes 393224 | tf_op jit(solution)/shard_map/ppermute | solution.py:427
  13.1 7.7 %collective-permute-start.9 = (bf16[256,256]{1,0:T(8,128)(2,1)S(1)}, bf16[256,256]{1,0:T(8,128)(2,1)S(1)}, u32[]{:S(2)}, u32[]{:S(2)}) collective-permute-start(bf16[256,256]{1,0:T(8,128)(2,1)S(1)} %collective-permute-done.8.ka_ref), channel_id=1, source_target_pairs={{8,0},{16,8},{24,16},{28,24},{20,28},{12,20},{4,12},{0,4},{9,1},{1... | collective-permute-start | bytes 393224 | tf_op jit(solution)/shard_map/ppermute | solution.py:427
  14.9 7.9 %collective-permute-start.6 = (bf16[256,256]{1,0:T(8,128)(2,1)S(1)}, bf16[256,256]{1,0:T(8,128)(2,1)S(1)}, u32[]{:S(2)}, u32[]{:S(2)}) collective-permute-start(bf16[256,256]{1,0:T(8,128)(2,1)S(1)} %collective-permute-done.5.va_ref), channel_id=1, source_target_pairs={{8,0},{16,8},{24,16},{28,24},{20,28},{12,20},{4,12},{0,4},{9,1},{1... | collective-permute-start | bytes 393224 | tf_op jit(solution)/shard_map/ppermute | solution.py:427
  16.5 8.0 %collective-permute-start.2 = (bf16[256,256]{1,0:T(8,128)(2,1)S(1)}, bf16[256,256]{1,0:T(8,128)(2,1)S(1)}, u32[]{:S(2)}, u32[]{:S(2)}) collective-permute-start(bf16[256,256]{1,0:T(8,128)(2,1)S(1)} %collective-permute-done.1.kb_ref), channel_id=1, source_target_pairs={{0,8},{8,16},{16,24},{24,28},{28,20},{20,12},{12,4},{4,0},{1,9},{9... | collective-permute-start | bytes 393224 | tf_op jit(solution)/shard_map/ppermute | solution.py:427
  19.6 10.2 %collective-permute-start.13 = (bf16[256,256]{1,0:T(8,128)(2,1)S(1)}, bf16[256,256]{1,0:T(8,128)(2,1)S(1)}, u32[]{:S(2)}, u32[]{:S(2)}) collective-permute-start(bf16[256,256]{1,0:T(8,128)(2,1)S(1)} %collective-permute-done.12.vb_ref), channel_id=1, source_target_pairs={{0,8},{8,16},{16,24},{24,28},{28,20},{20,12},{12,4},{4,0},{1,9},{9... | collective-permute-start | bytes 393224 | tf_op jit(solution)/shard_map/ppermute | solution.py:427
  20.8 9.0 %collective-permute-start.10 = (bf16[256,256]{1,0:T(8,128)(2,1)S(1)}, bf16[256,256]{1,0:T(8,128)(2,1)S(1)}, u32[]{:S(2)}, u32[]{:S(2)}) collective-permute-start(bf16[256,256]{1,0:T(8,128)(2,1)S(1)} %collective-permute-done.9.ka_ref), channel_id=1, source_target_pairs={{8,0},{16,8},{24,16},{28,24},{20,28},{12,20},{4,12},{0,4},{9,1},{1... | collective-permute-start | bytes 393224 | tf_op jit(solution)/shard_map/ppermute | solution.py:427
  22.8 9.4 %collective-permute-start.7 = (bf16[256,256]{1,0:T(8,128)(2,1)S(1)}, bf16[256,256]{1,0:T(8,128)(2,1)S(1)}, u32[]{:S(2)}, u32[]{:S(2)}) collective-permute-start(bf16[256,256]{1,0:T(8,128)(2,1)S(1)} %collective-permute-done.6.va_ref), channel_id=1, source_target_pairs={{8,0},{16,8},{24,16},{28,24},{20,28},{12,20},{4,12},{0,4},{9,1},{1... | collective-permute-start | bytes 393224 | tf_op jit(solution)/shard_map/ppermute | solution.py:427
  24.5 7.8 %collective-permute-start.3 = (bf16[256,256]{1,0:T(8,128)(2,1)S(1)}, bf16[256,256]{1,0:T(8,128)(2,1)S(1)}, u32[]{:S(2)}, u32[]{:S(2)}) collective-permute-start(bf16[256,256]{1,0:T(8,128)(2,1)S(1)} %collective-permute-done.2.kb_ref), channel_id=1, source_target_pairs={{0,8},{8,16},{16,24},{24,28},{28,20},{20,12},{12,4},{4,0},{1,9},{9... | collective-permute-start | bytes 393224 | tf_op jit(solution)/shard_map/ppermute | solution.py:427
  35.9 14.4 %collective-permute-start.14 = (bf16[256,256]{1,0:T(8,128)(2,1)S(1)}, bf16[256,256]{1,0:T(8,128)(2,1)S(1)}, u32[]{:S(2)}, u32[]{:S(2)}) collective-permute-start(bf16[256,256]{1,0:T(8,128)(2,1)S(1)} %get-tuple-element.62), channel_id=1, source_target_pairs={{0,8},{8,16},{16,24},{24,28},{28,20},{20,12},{12,4},{4,0},{1,9},{9... | collective-permute-start | bytes 393224 | tf_op jit(solution)/shard_map/ppermute | solution.py:427
  37.1 14.4 %collective-permute-start.24 = (bf16[256,256]{1,0:T(8,128)(2,1)S(1)}, bf16[256,256]{1,0:T(8,128)(2,1)S(1)}, u32[]{:S(2)}, u32[]{:S(2)}) collective-permute-start(bf16[256,256]{1,0:T(8,128)(2,1)S(1)} %get-tuple-element.73), channel_id=1, source_target_pairs={{8,0},{16,8},{24,16},{28,24},{20,28},{12,20},{4,12},{0,4},{9,1},{1... | collective-permute-start | bytes 393224 | tf_op jit(solution)/shard_map/ppermute | solution.py:427
  41.4 12.8 %collective-permute-start.21 = (bf16[256,256]{1,0:T(8,128)(2,1)S(1)}, bf16[256,256]{1,0:T(8,128)(2,1)S(1)}, u32[]{:S(2)}, u32[]{:S(2)}) collective-permute-start(bf16[256,256]{1,0:T(8,128)(2,1)S(1)} %convert_element_type.77), channel_id=1, source_target_pairs={{0,8},{8,16},{16,24},{24,28},{28,20},{20,12},{12,4},{4,0},{1,9},{9... | collective-permute-start | bytes 393224 | tf_op jit(solution)/shard_map/ppermute | solution.py:427
  42.6 9.9 %collective-permute-start.18 = (bf16[256,256]{1,0:T(8,128)(2,1)S(1)}, bf16[256,256]{1,0:T(8,128)(2,1)S(1)}, u32[]{:S(2)}, u32[]{:S(2)}) collective-permute-start(bf16[256,256]{1,0:T(8,128)(2,1)S(1)} %convert_element_type.72), channel_id=1, source_target_pairs={{8,0},{16,8},{24,16},{28,24},{20,28},{12,20},{4,12},{0,4},{9,1},{1... | collective-permute-start | bytes 393224 | tf_op jit(solution)/shard_map/ppermute | solution.py:427
  50.3 6.1 %collective-permute-start.15 = (bf16[256,256]{1,0:T(8,128)(2,1)S(1)}, bf16[256,256]{1,0:T(8,128)(2,1)S(1)}, u32[]{:S(2)}, u32[]{:S(2)}) collective-permute-start(bf16[256,256]{1,0:T(8,128)(2,1)S(1)} %add_convert_fusion.9), channel_id=1, source_target_pairs={{0,8},{8,16},{16,24},{24,28},{28,20},{20,12},{12,4},{4,0},{1,9},{9... | collective-permute-start | bytes 393224 | tf_op jit(solution)/shard_map/ppermute | solution.py:427
  52.5 6.5 %collective-permute-start.19 = (bf16[256,256]{1,0:T(8,128)(2,1)S(1)}, bf16[256,256]{1,0:T(8,128)(2,1)S(1)}, u32[]{:S(2)}, u32[]{:S(2)}) collective-permute-start(bf16[256,256]{1,0:T(8,128)(2,1)S(1)} %add_convert_fusion.6), channel_id=1, source_target_pairs={{8,0},{16,8},{24,16},{28,24},{20,28},{12,20},{4,12},{0,4},{9,1},{1... | collective-permute-start | bytes 393224 | tf_op jit(solution)/shard_map/ppermute | solution.py:427
  54.2 6.3 %collective-permute-start.22 = (bf16[256,256]{1,0:T(8,128)(2,1)S(1)}, bf16[256,256]{1,0:T(8,128)(2,1)S(1)}, u32[]{:S(2)}, u32[]{:S(2)}) collective-permute-start(bf16[256,256]{1,0:T(8,128)(2,1)S(1)} %add_convert_fusion.4), channel_id=1, source_target_pairs={{0,8},{8,16},{16,24},{24,28},{28,20},{20,12},{12,4},{4,0},{1,9},{9... | collective-permute-start | bytes 393224 | tf_op jit(solution)/shard_map/ppermute | solution.py:427
  59.1 9.0 %collective-permute-start.20 = (bf16[256,256]{1,0:T(8,128)(2,1)S(1)}, bf16[256,256]{1,0:T(8,128)(2,1)S(1)}, u32[]{:S(2)}, u32[]{:S(2)}) collective-permute-start(bf16[256,256]{1,0:T(8,128)(2,1)S(1)} %add_convert_fusion.5), channel_id=1, source_target_pairs={{8,0},{16,8},{24,16},{28,24},{20,28},{12,20},{4,12},{0,4},{9,1},{1... | collective-permute-start | bytes 393224 | tf_op jit(solution)/shard_map/ppermute | solution.py:427
  60.6 7.5 %collective-permute-start.23 = (bf16[256,256]{1,0:T(8,128)(2,1)S(1)}, bf16[256,256]{1,0:T(8,128)(2,1)S(1)}, u32[]{:S(2)}, u32[]{:S(2)}) collective-permute-start(bf16[256,256]{1,0:T(8,128)(2,1)S(1)} %add_convert_fusion.3), channel_id=1, source_target_pairs={{0,8},{8,16},{16,24},{24,28},{28,20},{20,12},{12,4},{4,0},{1,9},{9... | collective-permute-start | bytes 393224 | tf_op jit(solution)/shard_map/ppermute | solution.py:427
  61.6 6.6 %collective-permute-start.17 = (bf16[256,256]{1,0:T(8,128)(2,1)S(1)}, bf16[256,256]{1,0:T(8,128)(2,1)S(1)}, u32[]{:S(2)}, u32[]{:S(2)}) collective-permute-start(bf16[256,256]{1,0:T(8,128)(2,1)S(1)} %add_convert_fusion.7), channel_id=1, source_target_pairs={{0,8},{8,16},{16,24},{24,28},{28,20},{20,12},{12,4},{4,0},{1,9},{9... | collective-permute-start | bytes 393224 | tf_op jit(solution)/shard_map/ppermute | solution.py:427
  (10 other events, 36.8 us)

commit v3 on v2

--- a/solution.py
+++ b/solution.py
@@ -67,24 +67,33 @@
     return pl.ds(pl.multiple_of(index * size, size), size)
 
 
-def slot(w):
-    return w if isinstance(w, int) else jnp.maximum(w, 0)
-
-
-def block_of(ref, w, h):
-    return ref[at(slot(w), BLOCK), at(h, DH)]
-
-
-def key_of(ref, w, h, own):
-    return jnp.where(w >= 0, block_of(ref, w, h), own)
-
-
-def keep(w, x):
-    return jnp.where(w >= 0, x, jnp.zeros_like(x))
-
-
-def value_t(v, w):
-    return keep(w, jnp.concatenate([v.T, jnp.ones((2 * SUB, BLOCK), v.dtype)], axis=0))
+def block(ref, i, h):
+    return ref[i * BLOCK : (i + 1) * BLOCK, h * DH : (h + 1) * DH]
+
+
+def tall(tile):
+    return jnp.concatenate([tile] * (BLOCK // tile.shape[0]), axis=0)
+
+
+class Pick:
+    def __init__(self, table_ref, j, b):
+        self.count = table_ref.shape[2] - 1
+        self.tiles = [table_ref[j, b, i] for i in range(self.count + 1)]
+
+    def listed(self, ref, h):
+        terms = [block(ref, i, h) * tall(self.tiles[i]) for i in range(self.count)]
+        return functools.reduce(jnp.add, terms)
+
+    def key(self, ref, h, own):
+        return self.listed(ref, h) + own * tall(self.tiles[self.count])
+
+    def value_t(self, v):
+        return jnp.concatenate([v.T, functools.reduce(jnp.add, self.tiles[: self.count])], axis=0)
+
+    def add(self, ref, h, x):
+        for i in range(self.count):
+            factor = tall(self.tiles[i].astype(jnp.float32))
+            ref[i * BLOCK : (i + 1) * BLOCK, h * DH : (h + 1) * DH] += x * factor
 
 
 def queries_of(ref, b, h, part):
@@ -131,7 +140,7 @@
     )
 
 
-def table_kernel(slots_ref, counts_ref, tbl):
+def table_kernel(slots_ref, counts_ref, out_ref, tbl):
     blk_dev, n = tbl.shape
     me = lax.axis_index("ctx")
 
@@ -141,22 +150,27 @@
 
     for b in range(blk_dev):
         for j in range(n):
-            tbl[b, j] = -1
+            tbl[b, j] = blk_dev
         row = me * blk_dev + b
         for s in range(slots_ref.shape[0]):
-            block = slots_ref[s, row]
-            owner = lax.div(block, blk_dev)
+            listed = slots_ref[s, row]
+            owner = lax.div(listed, blk_dev)
             offset = lax.rem(place(owner) - place(me) + n, n)
 
             @pl.when(s < counts_ref[row])
             def _():
-                tbl[b, offset] = block - owner * blk_dev
+                tbl[b, offset] = listed - owner * blk_dev
+
+        for j in range(n):
+            for i in range(blk_dev + 1):
+                value = jnp.where(tbl[b, j] == i, 1.0, 0.0)
+                out_ref[j, b, i] = jnp.full((2 * SUB, DH), value, jnp.float32).astype(jnp.bfloat16)
 
 
 def table(blocks, counts, blk_dev, n):
     return call(
-        table_kernel, [SMEM] * 2, [jax.ShapeDtypeStruct((blk_dev, n), jnp.int32)], 1e10,
-        (blocks.T, counts), out_specs=[SMEM], size=1 << 26,
+        table_kernel, [SMEM] * 2, [bf16((n, blk_dev, blk_dev + 1, 2 * SUB, DH))], 1e10,
+        (blocks.T, counts), [pltpu.SMEM((blk_dev, n), jnp.int32)], size=1 << 26,
     )[0]
 
 
@@ -165,11 +179,11 @@
 
     def phases(c, part):
         b, h = c // heads, c % heads
-        k = block_of(k_ref, b, h)
-        x = dot_t(k, queries_of(q_ref, b, h, part))
+        x = dot_t(block(k_ref, b, h), queries_of(q_ref, b, h, part))
         turned = dot_t(unit, queries_of(o_ref, b, h, part))
         yield
-        v = value_t(block_of(v_ref, b, h), 0)
+        v = block(v_ref, b, h).T
+        v = jnp.concatenate([v, jnp.ones((2 * SUB, BLOCK), v.dtype)], axis=0)
         x = split(x * EXP2_SCALE)
         m = largest(x)
         m_ref[c, :, part] = m
@@ -196,13 +210,13 @@
 ):
     def phases(c, part):
         b, h = c // heads, c % heads
-        wa, wb = tbl[b, ja], tbl[b, jb]
-        own = block_of(own_ref, b, h)
-        k = jnp.concatenate([key_of(ka_ref, wa, h, own), key_of(kb_ref, wb, h, own)], axis=0)
+        pa, pb = Pick(tbl, ja, b), Pick(tbl, jb, b)
+        own = block(own_ref, b, h)
+        k = jnp.concatenate([pa.key(ka_ref, h, own), pb.key(kb_ref, h, own)], axis=0)
         x = dot_t(k, queries_of(q_ref, b, h, part))
         yield
         v = jnp.concatenate(
-            [value_t(block_of(va_ref, wa, h), wa), value_t(block_of(vb_ref, wb, h), wb)], axis=1
+            [pa.value_t(pa.listed(va_ref, h)), pb.value_t(pb.listed(vb_ref, h))], axis=1
         )
         x = split(x * EXP2_SCALE)
         old = m_in[c, :, part]
@@ -220,7 +234,7 @@
     combos = state[1].shape[0]
     return call(
         functools.partial(near_kernel, heads, ja, jb),
-        [SMEM] + [VMEM] * 8,
+        [VMEM] * 9,
         [f32(a.shape) for a in state],
         8 * combos * ROWS * BLOCK * DH,
         (tbl, q, k_own, *ahead, *behind, *state),
@@ -236,14 +250,14 @@
 
     def phases(c, part):
         b, h = c // heads, c % heads
-        w = tbl[b, opposite]
-        k = key_of(k_ref, w, h, block_of(own_ref, b, h))
-        v = block_of(v_ref, w, h)
+        pick = Pick(tbl, opposite, b)
+        k = pick.key(k_ref, h, block(own_ref, b, h))
+        v = pick.listed(v_ref, h)
         q, o = queries_of(q_ref, b, h, part), queries_of(o_ref, b, h, part)
         x = dot_t(k, q)
         yield
         grad_p = split(dot_t(v, o))
-        v_t = value_t(v, w)
+        v_t = pick.value_t(v)
         x = split(x * EXP2_SCALE)
         old = m_in[c, :, part]
         m = jnp.maximum(old, largest(x))
@@ -264,8 +278,8 @@
         lse_ref[c, :, part] = m + jnp.log2(total)
         delta_ref[c, :, part] = delta
         yield
-        pk_scr[at(slot(w), BLOCK), h * DH : (h + 1) * DH] += keep(w, dot(ds, q))
-        pv_scr[at(slot(w), BLOCK), h * DH : (h + 1) * DH] += keep(w, dot(weights, o))
+        pick.add(pk_scr, h, dot(ds, q))
+        pick.add(pv_scr, h, dot(weights, o))
 
     staggered(m_in.shape[0], TURN_PART, phases)
     pk_ref[...] = pk_scr[...].astype(jnp.bfloat16)
@@ -276,7 +290,7 @@
     combos = ot.shape[0]
     return call(
         functools.partial(turn_kernel, heads, opposite),
-        [SMEM] + [VMEM] * 8,
+        [VMEM] * 9,
         [bf16(ot.shape)]
         + [f32((combos, SUB, ROWS))] * 2
         + [bf16((combos, BLOCK, ROWS))]
@@ -305,23 +319,23 @@
 
     def phases(c, part):
         b, h = c // heads, c % heads
-        wa, wb = tbl[b, ja], tbl[b, jb]
-        own = block_of(own_ref, b, h)
-        ka, kb = key_of(ka_ref, wa, h, own), key_of(kb_ref, wb, h, own)
-        v = jnp.concatenate([block_of(va_ref, wa, h), block_of(vb_ref, wb, h)], axis=0)
+        pa, pb = Pick(tbl, ja, b), Pick(tbl, jb, b)
+        own = block(own_ref, b, h)
+        k = jnp.concatenate([pa.key(ka_ref, h, own), pb.key(kb_ref, h, own)], axis=0)
+        v = jnp.concatenate([pa.listed(va_ref, h), pb.listed(vb_ref, h)], axis=0)
         q, o = queries_of(q_ref, b, h, part), queries_of(o_ref, b, h, part)
-        x = dot_t(jnp.concatenate([ka, kb], axis=0), q)
+        x = dot_t(k, q)
         grad_p = dot_t(v, o)
         yield
         weights, ds = weights_and_grads(c, part, x, grad_p, lse_ref, delta_ref)
         yield
         dk, dv = dot(ds, q), dot(weights, o)
-        lanes = slice(h * DH, (h + 1) * DH)
-        for i, (rk, rv, w) in enumerate(((pka_ref, pva_ref, wa), (pkb_ref, pvb_ref, wb))):
+        for i, (pick, rk, rv) in enumerate(((pa, pka_ref, pva_ref), (pb, pkb_ref, pvb_ref))):
             src = slice(i * BLOCK, (i + 1) * BLOCK)
-            rk[at(slot(w), BLOCK), lanes] += keep(w, dk[src])
-            rv[at(slot(w), BLOCK), lanes] += keep(w, dv[src])
-        grad = dot(jnp.concatenate([keep(wa, ka).T, keep(wb, kb).T], axis=1), ds)
+            pick.add(rk, h, dk[src])
+            pick.add(rv, h, dv[src])
+        used = jnp.concatenate([pa.listed(ka_ref, h).T, pb.listed(kb_ref, h).T], axis=1)
+        grad = dot(used, ds)
         gq_ref[c, :, part] = gq_in[c, :, part] + grad if has_sum else grad
 
     staggered(gq_ref.shape[0], BACK_PART, phases)
@@ -332,7 +346,7 @@
     extra = () if gq is None else (gq,)
     return call(
         functools.partial(back_kernel, heads, ja, jb, gq is not None),
-        [SMEM] + [VMEM] * (9 + len(extra)),
+        [VMEM] * (10 + len(extra)),
         [f32(k_own.shape)] * 4 + [f32((combos, DH, ROWS))],
         20 * combos * ROWS * BLOCK * DH,
         (tbl, q, o, k_own, *stats, *ahead, *behind, *extra),
@@ -361,8 +375,8 @@
     def phases(c, part):
         b, h = c // heads, c % heads
         q, o = queries_of(q_ref, b, h, part), queries_of(o_ref, b, h, part)
-        k = block_of(k_ref, b, h)
-        x, grad_p = dot_t(k, q), dot_t(block_of(v_ref, b, h), o)
+        k = block(k_ref, b, h)
+        x, grad_p = dot_t(k, q), dot_t(block(v_ref, b, h), o)
         yield
         weights, ds = weights_and_grads(c, part, x, grad_p, lse_ref, delta_ref)
         put(att_scr, b, h, att_ref[c])
@@ -371,8 +385,7 @@
         place = (at(b, BLOCK), at(h, DH))
         pk_ref[place] = dot(ds, q)
         pv_ref[place] = dot(weights, o)
-        w4 = tbl[b, opposite]
-        used = jnp.concatenate([k.T, keep(w4, block_of(k4_ref, w4, h)).T], axis=1)
+        used = jnp.concatenate([k.T, Pick(tbl, opposite, b).listed(k4_ref, h).T], axis=1)
         grad = (gq_in[c] + dot(used, jnp.concatenate([ds, ds4_ref[c]], axis=0))) * SCALE
         yield
         put(gq_scr, b, h, grad.astype(jnp.bfloat16))
@@ -388,7 +401,7 @@
     combos = gq.shape[0]
     return call(
         functools.partial(own_kernel, heads, opposite),
-        [SMEM] + [VMEM] * 10,
+        [VMEM] * 11,
         [bf16(q.shape), bf16(q.shape), f32(k.shape), f32(k.shape)],
         12 * combos * ROWS * BLOCK * DH,
         (tbl, q, o, k, v, *stats, k4, ds4, att, gq),

time: 69.3 us -> 64.7 us (0.934)
  Pallas kernels: 28.4 us -> 22.9 us
  waiting for transfers between devices: 7.17 us -> 7.96 us
    pallas_call x11, Pallas kernels: 28.4 us -> 22.9 us  [call(): pl.pallas_call(kernel, in_specs=in_specs, out_specs=out_specs or [VMEM] *...]
    ppermute x28, waiting for transfers between devices: 7.17 us -> 7.96 us  [hop(): return lax.ppermute(x, 'ctx', ways[way])]
  transfers between devices with their start and end apart: 28 -> 28, of which waited for: 6 -> 6; matrix products, arithmetic and copies ran while one was open for 1% -> 0% of each run, Pallas kernels for 35% -> 30%
where the time goes in v3:
time: 64.7 us; the launch traced here: 64.5 us
  starting transfers between devices  31.1 us (48%)
  Pallas kernels  22.9 us (35%)
  waiting for transfers between devices  7.96 us (12%)
  local copies, waits for them, and re-layouts  1.36 us (2%)
  between operations  0.87 us (1%)
    ppermute x28, starting transfers between devices, hop(): return lax.ppermute(x, 'ctx', ways[way])  31.1 us
    pallas_call x11, Pallas kernels, call(): pl.pallas_call(kernel, in_specs=in_specs, out_specs=out_specs or [VMEM] *...  22.9 us
    ppermute x28, waiting for transfers between devices, hop(): return lax.ppermute(x, 'ctx', ways[way])  7.96 us
    unnamed x12, local copies, waits for them, and re-layouts  1.36 us
  transfers between devices with their start and end apart: 28, of which 6 were waited for; matrix products, arithmetic and copies ran while one was open for 0% of the time, Pallas kernels for 30%

profile of v3, /device:TPU:0, one launch (start us, length us, event | category | flops | bytes accessed | tf_op | source)
XLA Modules:
  0.0 64.5 jit_solution(7309049223435445621)
XLA Ops:
  0.6 3.0 %collective-permute-start.4 = (bf16[256,256]{1,0:T(8,128)(2,1)}, bf16[256,256]{1,0:T(8,128)(2,1)S(1)}, u32[]{:S(2)}, u32[]{:S(2)}) collective-permute-start(bf16[256,256]{1,0:T(8,128)(2,1)} %v_ref.3), channel_id=1, source_target_pairs={{8,0},{16,8},{24,16},{28,24},{20,28},{12,20},{4,12},{0,4},{9,1},{1... | collective-permute-start | bytes 393224 | tf_op jit(solution)/shard_map/ppermute | solution.py:440
  3.8 2.0 %collective-permute-start.11 = (bf16[256,256]{1,0:T(8,128)(2,1)}, bf16[256,256]{1,0:T(8,128)(2,1)S(1)}, u32[]{:S(2)}, u32[]{:S(2)}) collective-permute-start(bf16[256,256]{1,0:T(8,128)(2,1)} %v_ref.3), channel_id=1, source_target_pairs={{0,8},{8,16},{16,24},{24,28},{28,20},{20,12},{12,4},{4,0},{1,9},{9... | collective-permute-start | bytes 393224 | tf_op jit(solution)/shard_map/ppermute | solution.py:440
  5.8 2.0 %collective-permute-done.4.va_ref = bf16[256,256]{1,0:T(8,128)(2,1)S(1)} collective-permute-done((bf16[256,256]{1,0:T(8,128)(2,1)}, bf16[256,256]{1,0:T(8,128)(2,1)S(1)}, u32[]{:S(2)}, u32[]{:S(2)}) %collective-permute-start.4) | collective-permute-done | bytes 131104 | tf_op jit(solution)/shard_map/ppermute | solution.py:440
  7.9 2.4 %collective-permute-start.5 = (bf16[256,256]{1,0:T(8,128)(2,1)S(1)}, bf16[256,256]{1,0:T(8,128)(2,1)S(1)}, u32[]{:S(2)}, u32[]{:S(2)}) collective-permute-start(bf16[256,256]{1,0:T(8,128)(2,1)S(1)} %collective-permute-done.4.va_ref), channel_id=1, source_target_pairs={{8,0},{16,8},{24,16},{28,24},{20,28},{12,20},{4,12},{0,4},{9,1},{1... | collective-permute-start | bytes 393224 | tf_op jit(solution)/shard_map/ppermute | solution.py:440
  10.4 2.5 %collective-permute-done.11.vb_ref = bf16[256,256]{1,0:T(8,128)(2,1)S(1)} collective-permute-done((bf16[256,256]{1,0:T(8,128)(2,1)}, bf16[256,256]{1,0:T(8,128)(2,1)S(1)}, u32[]{:S(2)}, u32[]{:S(2)}) %collective-permute-start.11) | collective-permute-done | bytes 131104 | tf_op jit(solution)/shard_map/ppermute | solution.py:440
  13.1 1.8 %collective-permute-start.9 = (bf16[256,256]{1,0:T(8,128)(2,1)S(1)}, bf16[256,256]{1,0:T(8,128)(2,1)S(1)}, u32[]{:S(2)}, u32[]{:S(2)}) collective-permute-start(bf16[256,256]{1,0:T(8,128)(2,1)S(1)} %collective-permute-done.8.ka_ref), channel_id=1, source_target_pairs={{8,0},{16,8},{24,16},{28,24},{20,28},{12,20},{4,12},{0,4},{9,1},{1... | collective-permute-start | bytes 393224 | tf_op jit(solution)/shard_map/ppermute | solution.py:440
  14.9 1.6 %collective-permute-start.6 = (bf16[256,256]{1,0:T(8,128)(2,1)S(1)}, bf16[256,256]{1,0:T(8,128)(2,1)S(1)}, u32[]{:S(2)}, u32[]{:S(2)}) collective-permute-start(bf16[256,256]{1,0:T(8,128)(2,1)S(1)} %collective-permute-done.5.va_ref), channel_id=1, source_target_pairs={{8,0},{16,8},{24,16},{28,24},{20,28},{12,20},{4,12},{0,4},{9,1},{1... | collective-permute-start | bytes 393224 | tf_op jit(solution)/shard_map/ppermute | solution.py:440
  22.3 1.7 %collective-permute-start.7 = (bf16[256,256]{1,0:T(8,128)(2,1)S(1)}, bf16[256,256]{1,0:T(8,128)(2,1)S(1)}, u32[]{:S(2)}, u32[]{:S(2)}) collective-permute-start(bf16[256,256]{1,0:T(8,128)(2,1)S(1)} %collective-permute-done.6.va_ref), channel_id=1, source_target_pairs={{8,0},{16,8},{24,16},{28,24},{20,28},{12,20},{4,12},{0,4},{9,1},{1... | collective-permute-start | bytes 393224 | tf_op jit(solution)/shard_map/ppermute | solution.py:440
  24.3 1.9 %shard_map.95 = (f32[4,136,1024]{2,1,0:T(8,128)S(1)}, f32[4,8,1024]{2,1,0:T(8,128)S(1)}) custom-call(bf16[8,2,3,16,128]{4,3,2,1,0:T(8,128)(2,1)S(1)} %shard_map.93.tbl, bf16[256,2048]{1,0:T(8,128)(2,1)S(1)} %copy-done, bf16[256,256]{1,0:T(8,128)(2,1)S(1)} %copy-done.2, bf16[256,256]{1,0:T(8,128)(2,1)S(1)} %collective-permute-done.8.ka_ref, ...), custom_call_target="tpu_custom_call" | custom-call | flops 536870912 | bytes 1048576 | tf_op jit(solution)/shard_map/pallas_call | solution.py:51
  26.3 1.9 %shard_map.96 = (f32[4,136,1024]{2,1,0:T(8,128)S(1)}, f32[4,8,1024]{2,1,0:T(8,128)S(1)}) custom-call(bf16[8,2,3,16,128]{4,3,2,1,0:T(8,128)(2,1)S(1)} %shard_map.93.tbl, bf16[256,2048]{1,0:T(8,128)(2,1)S(1)} %copy-done, bf16[256,256]{1,0:T(8,128)(2,1)S(1)} %copy-done.2, bf16[256,256]{1,0:T(8,128)(2,1)S(1)} %collective-permute-done.9.ka_ref, ...), custom_call_target="tpu_custom_call" | custom-call | flops 536870912 | bytes 1048576 | tf_op jit(solution)/shard_map/pallas_call | solution.py:51
  28.2 1.9 %shard_map.97 = (f32[4,136,1024]{2,1,0:T(8,128)S(1)}, f32[4,8,1024]{2,1,0:T(8,128)S(1)}) custom-call(bf16[8,2,3,16,128]{4,3,2,1,0:T(8,128)(2,1)S(1)} %shard_map.93.tbl, bf16[256,2048]{1,0:T(8,128)(2,1)S(1)} %copy-done, bf16[256,256]{1,0:T(8,128)(2,1)S(1)} %copy-done.2, bf16[256,256]{1,0:T(8,128)(2,1)S(1)} %collective-permute-done.10.ka_ref, ...), custom_call_target="tpu_custom_call" | custom-call | flops 536870912 | bytes 1048576 | tf_op jit(solution)/shard_map/pallas_call | solution.py:51
  30.1 2.9 %shard_map.98 = (bf16[4,128,1024]{2,1,0:T(8,128)(2,1)S(1)}, f32[4,8,1024]{2,1,0:T(8,128)S(1)}, f32[4,8,1024]{2,1,0:T(8,128)S(1)}, bf16[4,128,1024]{2,1,0:T(8,128...) custom-call(bf16[8,2,3,16,128]{4,3,2,1,0:T(8,128)(2,1)S(1)} %shard_map.93.tbl, ...), custom_call_target="tpu_custom_call" | custom-call | flops 671088640 | bytes 1048576 | tf_op jit(solution)/shard_map/pallas_call | solution.py:51
  33.0 1.2 %collective-permute-start.14 = (bf16[256,256]{1,0:T(8,128)(2,1)S(1)}, bf16[256,256]{1,0:T(8,128)(2,1)S(1)}, u32[]{:S(2)}, u32[]{:S(2)}) collective-permute-start(bf16[256,256]{1,0:T(8,128)(2,1)S(1)} %get-tuple-element.62), channel_id=1, source_target_pairs={{0,8},{8,16},{16,24},{24,28},{28,20},{20,12},{12,4},{4,0},{1,9},{9... | collective-permute-start | bytes 393224 | tf_op jit(solution)/shard_map/ppermute | solution.py:440
  35.1 2.7 %shard_map.99 = (f32[256,256]{1,0:T(8,128)S(1)}, f32[256,256]{1,0:T(8,128)S(1)}, f32[256,256]{1,0:T(8,128)S(1)}, f32[256,256]{1,0:T(8,128)S(1)}, f32[4,128,1024]{2,1,0:T(8,128)S(1)}) custom-call(bf16[8,2,3,16,128]{4,3,2,1,0:T(8,128)(2,1)S(1)} %shard_map.93.tbl, bf16[256,2048]{1,0:T(8,128)(2,1)S(1)} %copy-done, bf16[256,2048]{1,0:T(8,128)(2,1)S(1)} %copy-done.1, ...), custom_call_target="tpu_custom_call" | custom-call | flops 1342177280 | bytes 1048576 | tf_op jit(solution)/shard_map/pallas_call | solution.py:51
  37.9 1.2 %collective-permute-start.21 = (bf16[256,256]{1,0:T(8,128)(2,1)S(1)}, bf16[256,256]{1,0:T(8,128)(2,1)S(1)}, u32[]{:S(2)}, u32[]{:S(2)}) collective-permute-start(bf16[256,256]{1,0:T(8,128)(2,1)S(1)} %convert_element_type.77), channel_id=1, source_target_pairs={{0,8},{8,16},{16,24},{24,28},{28,20},{20,12},{12,4},{4,0},{1,9},{9... | collective-permute-start | bytes 393224 | tf_op jit(solution)/shard_map/ppermute | solution.py:440
  39.9 2.7 %shard_map.100 = (f32[256,256]{1,0:T(8,128)S(1)}, f32[256,256]{1,0:T(8,128)S(1)}, f32[256,256]{1,0:T(8,128)S(1)}, f32[256,256]{1,0:T(8,128)S(1)}, f32[4,128,1024]{2,1,0:T(8,128)S(1)}) custom-call(bf16[8,2,3,16,128]{4,3,2,1,0:T(8,128)(2,1)S(1)} %shard_map.93.tbl, bf16[256,2048]{1,0:T(8,128)(2,1)S(1)} %copy-done, bf16[256,2048]{1,0:T(8,128)(2,1)S(1)} %copy-done.1, ...), custom_call_target="tpu_custom_call" | custom-call | flops 1342177280 | bytes 1048576 | tf_op jit(solution)/shard_map/pallas_call | solution.py:51
  42.7 2.7 %shard_map.101 = (f32[256,256]{1,0:T(8,128)S(1)}, f32[256,256]{1,0:T(8,128)S(1)}, f32[256,256]{1,0:T(8,128)S(1)}, f32[256,256]{1,0:T(8,128)S(1)}, f32[4,128,1024]{2,1,0:T(8,128)S(1)}) custom-call(bf16[8,2,3,16,128]{4,3,2,1,0:T(8,128)(2,1)S(1)} %shard_map.93.tbl, bf16[256,2048]{1,0:T(8,128)(2,1)S(1)} %copy-done, bf16[256,2048]{1,0:T(8,128)(2,1)S(1)} %copy-done.1, ...), custom_call_target="tpu_custom_call" | custom-call | flops 1342177280 | bytes 1048576 | tf_op jit(solution)/shard_map/pallas_call | solution.py:51
  45.4 1.2 %collective-permute-start.15 = (bf16[256,256]{1,0:T(8,128)(2,1)S(1)}, bf16[256,256]{1,0:T(8,128)(2,1)S(1)}, u32[]{:S(2)}, u32[]{:S(2)}) collective-permute-start(bf16[256,256]{1,0:T(8,128)(2,1)S(1)} %add_convert_fusion.9), channel_id=1, source_target_pairs={{0,8},{8,16},{16,24},{24,28},{28,20},{20,12},{12,4},{4,0},{1,9},{9... | collective-permute-start | bytes 393224 | tf_op jit(solution)/shard_map/ppermute | solution.py:440
  47.6 1.7 %collective-permute-start.19 = (bf16[256,256]{1,0:T(8,128)(2,1)S(1)}, bf16[256,256]{1,0:T(8,128)(2,1)S(1)}, u32[]{:S(2)}, u32[]{:S(2)}) collective-permute-start(bf16[256,256]{1,0:T(8,128)(2,1)S(1)} %add_convert_fusion.6), channel_id=1, source_target_pairs={{8,0},{16,8},{24,16},{28,24},{20,28},{12,20},{4,12},{0,4},{9,1},{1... | collective-permute-start | bytes 393224 | tf_op jit(solution)/shard_map/ppermute | solution.py:440
  50.9 1.2 %collective-permute-start.16 = (bf16[256,256]{1,0:T(8,128)(2,1)S(1)}, bf16[256,256]{1,0:T(8,128)(2,1)S(1)}, u32[]{:S(2)}, u32[]{:S(2)}) collective-permute-start(bf16[256,256]{1,0:T(8,128)(2,1)S(1)} %add_convert_fusion.8), channel_id=1, source_target_pairs={{0,8},{8,16},{16,24},{24,28},{28,20},{20,12},{12,4},{4,0},{1,9},{9... | collective-permute-start | bytes 393224 | tf_op jit(solution)/shard_map/ppermute | solution.py:440
  53.3 1.4 %collective-permute-done.19 = bf16[256,256]{1,0:T(8,128)(2,1)S(1)} collective-permute-done((bf16[256,256]{1,0:T(8,128)(2,1)S(1)}, bf16[256,256]{1,0:T(8,128)(2,1)S(1)}, u32[]{:S(2)}, u32[]{:S(2)}) %collective-permute-start.19) | collective-permute-done | bytes 131104 | tf_op jit(solution)/shard_map/ppermute | solution.py:440
  54.7 1.3 %collective-permute-start.20 = (bf16[256,256]{1,0:T(8,128)(2,1)S(1)}, bf16[256,256]{1,0:T(8,128)(2,1)S(1)}, u32[]{:S(2)}, u32[]{:S(2)}) collective-permute-start(bf16[256,256]{1,0:T(8,128)(2,1)S(1)} %add_convert_fusion.5), channel_id=1, source_target_pairs={{8,0},{16,8},{24,16},{28,24},{20,28},{12,20},{4,12},{0,4},{9,1},{1... | collective-permute-start | bytes 393224 | tf_op jit(solution)/shard_map/ppermute | solution.py:440
  56.9 1.5 %collective-permute-start.17 = (bf16[256,256]{1,0:T(8,128)(2,1)S(1)}, bf16[256,256]{1,0:T(8,128)(2,1)S(1)}, u32[]{:S(2)}, u32[]{:S(2)}) collective-permute-start(bf16[256,256]{1,0:T(8,128)(2,1)S(1)} %add_convert_fusion.7), channel_id=1, source_target_pairs={{0,8},{8,16},{16,24},{24,28},{28,20},{20,12},{12,4},{4,0},{1,9},{9... | collective-permute-start | bytes 393224 | tf_op jit(solution)/shard_map/ppermute | solution.py:440
  59.3 3.5 %shard_map.102 = (bf16[256,2048]{1,0:T(8,128)(2,1)}, bf16[256,2048]{1,0:T(8,128)(2,1)}, f32[256,256]{1,0:T(8,128)S(1)}, f32[256,256]{1,0:T(8,128)S(1)}) custom-call(bf16[8,2,3,16,128]{4,3,2,1,0:T(8,128)(2,1)S(1)} %shard_map.93.tbl, bf16[256,2048]{1,0:T(8,128)(2,1)S(1)} %copy-done, bf16[256,2048]{1,0:T(8,128)(2,1)S(1)} %copy-done.1, ...), custom_call_target="tpu_custom_call" | custom-call | flops 805306368 | bytes 1048576 | tf_op jit(solution)/shard_map/pallas_call | solution.py:51
  (67 shorter events, 15.6 us)
Async XLA Ops:
  0.6 7.2 %collective-permute-start.4 = (bf16[256,256]{1,0:T(8,128)(2,1)}, bf16[256,256]{1,0:T(8,128)(2,1)S(1)}, u32[]{:S(2)}, u32[]{:S(2)}) collective-permute-start(bf16[256,256]{1,0:T(8,128)(2,1)} %v_ref.3), channel_id=1, source_target_pairs={{8,0},{16,8},{24,16},{28,24},{20,28},{12,20},{4,12},{0,4},{9,1},{1... | collective-permute-start | bytes 393224 | tf_op jit(solution)/shard_map/ppermute | solution.py:440
  3.7 6.6 %collective-permute-start = (bf16[256,256]{1,0:T(8,128)(2,1)}, bf16[256,256]{1,0:T(8,128)(2,1)S(1)}, u32[]{:S(2)}, u32[]{:S(2)}) collective-permute-start(bf16[256,256]{1,0:T(8,128)(2,1)} %k_ref.3), channel_id=1, source_target_pairs={{0,8},{8,16},{16,24},{24,28},{28,20},{20,12},{12,4},{4,0},{1,9},{9... | collective-permute-start | bytes 393224 | tf_op jit(solution)/shard_map/ppermute | solution.py:440
  3.8 9.1 %collective-permute-start.11 = (bf16[256,256]{1,0:T(8,128)(2,1)}, bf16[256,256]{1,0:T(8,128)(2,1)S(1)}, u32[]{:S(2)}, u32[]{:S(2)}) collective-permute-start(bf16[256,256]{1,0:T(8,128)(2,1)} %v_ref.3), channel_id=1, source_target_pairs={{0,8},{8,16},{16,24},{24,28},{28,20},{20,12},{12,4},{4,0},{1,9},{9... | collective-permute-start | bytes 393224 | tf_op jit(solution)/shard_map/ppermute | solution.py:440
  5.8 7.3 %collective-permute-start.8 = (bf16[256,256]{1,0:T(8,128)(2,1)}, bf16[256,256]{1,0:T(8,128)(2,1)S(1)}, u32[]{:S(2)}, u32[]{:S(2)}) collective-permute-start(bf16[256,256]{1,0:T(8,128)(2,1)} %k_ref.3), channel_id=1, source_target_pairs={{8,0},{16,8},{24,16},{28,24},{20,28},{12,20},{4,12},{0,4},{9,1},{1... | collective-permute-start | bytes 393224 | tf_op jit(solution)/shard_map/ppermute | solution.py:440
  7.9 7.0 %collective-permute-start.5 = (bf16[256,256]{1,0:T(8,128)(2,1)S(1)}, bf16[256,256]{1,0:T(8,128)(2,1)S(1)}, u32[]{:S(2)}, u32[]{:S(2)}) collective-permute-start(bf16[256,256]{1,0:T(8,128)(2,1)S(1)} %collective-permute-done.4.va_ref), channel_id=1, source_target_pairs={{8,0},{16,8},{24,16},{28,24},{20,28},{12,20},{4,12},{0,4},{9,1},{1... | collective-permute-start | bytes 393224 | tf_op jit(solution)/shard_map/ppermute | solution.py:440
  10.2 6.2 %collective-permute-start.1 = (bf16[256,256]{1,0:T(8,128)(2,1)S(1)}, bf16[256,256]{1,0:T(8,128)(2,1)S(1)}, u32[]{:S(2)}, u32[]{:S(2)}) collective-permute-start(bf16[256,256]{1,0:T(8,128)(2,1)S(1)} %collective-permute-done.kb_ref), channel_id=1, source_target_pairs={{0,8},{8,16},{16,24},{24,28},{28,20},{20,12},{12,4},{4,0},{1,9},{9... | collective-permute-start | bytes 393224 | tf_op jit(solution)/shard_map/ppermute | solution.py:440
  12.9 6.2 %collective-permute-start.12 = (bf16[256,256]{1,0:T(8,128)(2,1)S(1)}, bf16[256,256]{1,0:T(8,128)(2,1)S(1)}, u32[]{:S(2)}, u32[]{:S(2)}) collective-permute-start(bf16[256,256]{1,0:T(8,128)(2,1)S(1)} %collective-permute-done.11.vb_ref), channel_id=1, source_target_pairs={{0,8},{8,16},{16,24},{24,28},{28,20},{20,12},{12,4},{4,0},{1,9},{9... | collective-permute-start | bytes 393224 | tf_op jit(solution)/shard_map/ppermute | solution.py:440
  13.1 7.2 %collective-permute-start.9 = (bf16[256,256]{1,0:T(8,128)(2,1)S(1)}, bf16[256,256]{1,0:T(8,128)(2,1)S(1)}, u32[]{:S(2)}, u32[]{:S(2)}) collective-permute-start(bf16[256,256]{1,0:T(8,128)(2,1)S(1)} %collective-permute-done.8.ka_ref), channel_id=1, source_target_pairs={{8,0},{16,8},{24,16},{28,24},{20,28},{12,20},{4,12},{0,4},{9,1},{1... | collective-permute-start | bytes 393224 | tf_op jit(solution)/shard_map/ppermute | solution.py:440
  14.9 7.4 %collective-permute-start.6 = (bf16[256,256]{1,0:T(8,128)(2,1)S(1)}, bf16[256,256]{1,0:T(8,128)(2,1)S(1)}, u32[]{:S(2)}, u32[]{:S(2)}) collective-permute-start(bf16[256,256]{1,0:T(8,128)(2,1)S(1)} %collective-permute-done.5.va_ref), channel_id=1, source_target_pairs={{8,0},{16,8},{24,16},{28,24},{20,28},{12,20},{4,12},{0,4},{9,1},{1... | collective-permute-start | bytes 393224 | tf_op jit(solution)/shard_map/ppermute | solution.py:440
  16.5 7.5 %collective-permute-start.2 = (bf16[256,256]{1,0:T(8,128)(2,1)S(1)}, bf16[256,256]{1,0:T(8,128)(2,1)S(1)}, u32[]{:S(2)}, u32[]{:S(2)}) collective-permute-start(bf16[256,256]{1,0:T(8,128)(2,1)S(1)} %collective-permute-done.1.kb_ref), channel_id=1, source_target_pairs={{0,8},{8,16},{16,24},{24,28},{28,20},{20,12},{12,4},{4,0},{1,9},{9... | collective-permute-start | bytes 393224 | tf_op jit(solution)/shard_map/ppermute | solution.py:440
  19.1 9.1 %collective-permute-start.13 = (bf16[256,256]{1,0:T(8,128)(2,1)S(1)}, bf16[256,256]{1,0:T(8,128)(2,1)S(1)}, u32[]{:S(2)}, u32[]{:S(2)}) collective-permute-start(bf16[256,256]{1,0:T(8,128)(2,1)S(1)} %collective-permute-done.12.vb_ref), channel_id=1, source_target_pairs={{0,8},{8,16},{16,24},{24,28},{28,20},{20,12},{12,4},{4,0},{1,9},{9... | collective-permute-start | bytes 393224 | tf_op jit(solution)/shard_map/ppermute | solution.py:440
  20.2 7.9 %collective-permute-start.10 = (bf16[256,256]{1,0:T(8,128)(2,1)S(1)}, bf16[256,256]{1,0:T(8,128)(2,1)S(1)}, u32[]{:S(2)}, u32[]{:S(2)}) collective-permute-start(bf16[256,256]{1,0:T(8,128)(2,1)S(1)} %collective-permute-done.9.ka_ref), channel_id=1, source_target_pairs={{8,0},{16,8},{24,16},{28,24},{20,28},{12,20},{4,12},{0,4},{9,1},{1... | collective-permute-start | bytes 393224 | tf_op jit(solution)/shard_map/ppermute | solution.py:440
  22.3 7.9 %collective-permute-start.7 = (bf16[256,256]{1,0:T(8,128)(2,1)S(1)}, bf16[256,256]{1,0:T(8,128)(2,1)S(1)}, u32[]{:S(2)}, u32[]{:S(2)}) collective-permute-start(bf16[256,256]{1,0:T(8,128)(2,1)S(1)} %collective-permute-done.6.va_ref), channel_id=1, source_target_pairs={{8,0},{16,8},{24,16},{28,24},{20,28},{12,20},{4,12},{0,4},{9,1},{1... | collective-permute-start | bytes 393224 | tf_op jit(solution)/shard_map/ppermute | solution.py:440
  24.0 6.1 %collective-permute-start.3 = (bf16[256,256]{1,0:T(8,128)(2,1)S(1)}, bf16[256,256]{1,0:T(8,128)(2,1)S(1)}, u32[]{:S(2)}, u32[]{:S(2)}) collective-permute-start(bf16[256,256]{1,0:T(8,128)(2,1)S(1)} %collective-permute-done.2.kb_ref), channel_id=1, source_target_pairs={{0,8},{8,16},{16,24},{24,28},{28,20},{20,12},{12,4},{4,0},{1,9},{9... | collective-permute-start | bytes 393224 | tf_op jit(solution)/shard_map/ppermute | solution.py:440
  33.0 12.4 %collective-permute-start.14 = (bf16[256,256]{1,0:T(8,128)(2,1)S(1)}, bf16[256,256]{1,0:T(8,128)(2,1)S(1)}, u32[]{:S(2)}, u32[]{:S(2)}) collective-permute-start(bf16[256,256]{1,0:T(8,128)(2,1)S(1)} %get-tuple-element.62), channel_id=1, source_target_pairs={{0,8},{8,16},{16,24},{24,28},{28,20},{20,12},{12,4},{4,0},{1,9},{9... | collective-permute-start | bytes 393224 | tf_op jit(solution)/shard_map/ppermute | solution.py:440
  34.2 12.4 %collective-permute-start.24 = (bf16[256,256]{1,0:T(8,128)(2,1)S(1)}, bf16[256,256]{1,0:T(8,128)(2,1)S(1)}, u32[]{:S(2)}, u32[]{:S(2)}) collective-permute-start(bf16[256,256]{1,0:T(8,128)(2,1)S(1)} %get-tuple-element.73), channel_id=1, source_target_pairs={{8,0},{16,8},{24,16},{28,24},{20,28},{12,20},{4,12},{0,4},{9,1},{1... | collective-permute-start | bytes 393224 | tf_op jit(solution)/shard_map/ppermute | solution.py:440
  37.9 11.5 %collective-permute-start.21 = (bf16[256,256]{1,0:T(8,128)(2,1)S(1)}, bf16[256,256]{1,0:T(8,128)(2,1)S(1)}, u32[]{:S(2)}, u32[]{:S(2)}) collective-permute-start(bf16[256,256]{1,0:T(8,128)(2,1)S(1)} %convert_element_type.77), channel_id=1, source_target_pairs={{0,8},{8,16},{16,24},{24,28},{28,20},{20,12},{12,4},{4,0},{1,9},{9... | collective-permute-start | bytes 393224 | tf_op jit(solution)/shard_map/ppermute | solution.py:440
  39.0 8.6 %collective-permute-start.18 = (bf16[256,256]{1,0:T(8,128)(2,1)S(1)}, bf16[256,256]{1,0:T(8,128)(2,1)S(1)}, u32[]{:S(2)}, u32[]{:S(2)}) collective-permute-start(bf16[256,256]{1,0:T(8,128)(2,1)S(1)} %convert_element_type.72), channel_id=1, source_target_pairs={{8,0},{16,8},{24,16},{28,24},{20,28},{12,20},{4,12},{0,4},{9,1},{1... | collective-permute-start | bytes 393224 | tf_op jit(solution)/shard_map/ppermute | solution.py:440
  47.6 7.1 %collective-permute-start.19 = (bf16[256,256]{1,0:T(8,128)(2,1)S(1)}, bf16[256,256]{1,0:T(8,128)(2,1)S(1)}, u32[]{:S(2)}, u32[]{:S(2)}) collective-permute-start(bf16[256,256]{1,0:T(8,128)(2,1)S(1)} %add_convert_fusion.6), channel_id=1, source_target_pairs={{8,0},{16,8},{24,16},{28,24},{20,28},{12,20},{4,12},{0,4},{9,1},{1... | collective-permute-start | bytes 393224 | tf_op jit(solution)/shard_map/ppermute | solution.py:440
  49.4 6.6 %collective-permute-start.22 = (bf16[256,256]{1,0:T(8,128)(2,1)S(1)}, bf16[256,256]{1,0:T(8,128)(2,1)S(1)}, u32[]{:S(2)}, u32[]{:S(2)}) collective-permute-start(bf16[256,256]{1,0:T(8,128)(2,1)S(1)} %add_convert_fusion.4), channel_id=1, source_target_pairs={{0,8},{8,16},{16,24},{24,28},{28,20},{20,12},{12,4},{4,0},{1,9},{9... | collective-permute-start | bytes 393224 | tf_op jit(solution)/shard_map/ppermute | solution.py:440
  50.9 6.0 %collective-permute-start.16 = (bf16[256,256]{1,0:T(8,128)(2,1)S(1)}, bf16[256,256]{1,0:T(8,128)(2,1)S(1)}, u32[]{:S(2)}, u32[]{:S(2)}) collective-permute-start(bf16[256,256]{1,0:T(8,128)(2,1)S(1)} %add_convert_fusion.8), channel_id=1, source_target_pairs={{0,8},{8,16},{16,24},{24,28},{28,20},{20,12},{12,4},{4,0},{1,9},{9... | collective-permute-start | bytes 393224 | tf_op jit(solution)/shard_map/ppermute | solution.py:440
  52.3 6.2 %collective-permute-start.26 = (bf16[256,256]{1,0:T(8,128)(2,1)S(1)}, bf16[256,256]{1,0:T(8,128)(2,1)S(1)}, u32[]{:S(2)}, u32[]{:S(2)}) collective-permute-start(bf16[256,256]{1,0:T(8,128)(2,1)S(1)} %add_convert_fusion.1), channel_id=1, source_target_pairs={{8,0},{16,8},{24,16},{28,24},{20,28},{12,20},{4,12},{0,4},{9,1},{1... | collective-permute-start | bytes 393224 | tf_op jit(solution)/shard_map/ppermute | solution.py:440
  54.7 8.1 %collective-permute-start.20 = (bf16[256,256]{1,0:T(8,128)(2,1)S(1)}, bf16[256,256]{1,0:T(8,128)(2,1)S(1)}, u32[]{:S(2)}, u32[]{:S(2)}) collective-permute-start(bf16[256,256]{1,0:T(8,128)(2,1)S(1)} %add_convert_fusion.5), channel_id=1, source_target_pairs={{8,0},{16,8},{24,16},{28,24},{20,28},{12,20},{4,12},{0,4},{9,1},{1... | collective-permute-start | bytes 393224 | tf_op jit(solution)/shard_map/ppermute | solution.py:440
  56.0 6.8 %collective-permute-start.23 = (bf16[256,256]{1,0:T(8,128)(2,1)S(1)}, bf16[256,256]{1,0:T(8,128)(2,1)S(1)}, u32[]{:S(2)}, u32[]{:S(2)}) collective-permute-start(bf16[256,256]{1,0:T(8,128)(2,1)S(1)} %add_convert_fusion.3), channel_id=1, source_target_pairs={{0,8},{8,16},{16,24},{24,28},{28,20},{20,12},{12,4},{4,0},{1,9},{9... | collective-permute-start | bytes 393224 | tf_op jit(solution)/shard_map/ppermute | solution.py:440
  (10 other events, 35.0 us)
